TPU v7x, 256 devices: a whole 4x4x8 slice. The times are simulated.
256 devices in a mesh: gx: 16 (over z, x_lo), gy: 4 (over x_hi, core), gz: 4 (over y).
Axes of the slice: x: 4 (x_hi: 2, x_lo: 2; x = x_hi * 2 + x_lo), y: 4, z: 8, core: 2. Of those that a mesh axis runs over, the one named last changes fastest.
Arguments:
- velocity: float32 [3, 256, 64, 1024], P(None, 'gx', 'gy', 'gz'), may hold values from -24 to 24
- metric: float32 [3, 256, 64, 1024], P(None, 'gx', 'gy', 'gz'), may hold values from 0.5 to 2
Outputs:
- viscosity: float32 [256, 64, 1024], P('gx', 'gy', 'gz')
- coefficient: float32 [256, 64], P('gx', 'gy')
All inputs are finite; a program needn't handle non-finite values.
Results may differ from a plain program's by a relative error of at most 0.0003.
Values sent between devices are 32-bit elements; how exact they have to be, the bound alone decides.
A program may use at most 64 MiB of HBM per device.

v0:
```python
import jax
import jax.numpy as jnp
from jax import lax
from jax.sharding import PartitionSpec as P

pair_rows = (0, 1, 2, 0, 0, 1)
pair_cols = (0, 1, 2, 1, 2, 2)
pair_weight = (1.0, 1.0, 1.0, 2.0, 2.0, 2.0)
eps_line = 1e-06
ratio_square = 4.0


def with_halo(block, sides, width, periodic):
    for axis, dim in sides:
        count = lax.axis_size(axis)
        forward = [(i, i + 1) for i in range(count - 1)]
        if periodic:
            forward.append((count - 1, 0))
        backward = [(target, source) for source, target in forward]
        low = lax.ppermute(
            lax.slice_in_dim(block, block.shape[dim] - width, None, axis=dim), axis, forward
        )
        high = lax.ppermute(lax.slice_in_dim(block, 0, width, axis=dim), axis, backward)
        block = jnp.concatenate([low, block, high], axis=dim)
    return block


def with_halo_2(x, sides, width):
    edges = {}
    for axis, dim in sides:
        count, length = (lax.axis_size(axis), x.shape[dim])
        up = [(i, (i + 1) % count) for i in range(count - 1)]
        last = lax.slice_in_dim(x, length - width, length, axis=dim)
        leading = lax.slice_in_dim(x, 0, width, axis=dim)
        edges[dim] = (
            lax.ppermute(last, axis, up),
            lax.ppermute(leading, axis, [(b, a) for a, b in up]),
        )
    done = []
    for _, dim in sides:
        low, high = edges[dim]
        around = [(width, width) if d in done else (0, 0) for d in range(x.ndim)]
        x = jnp.concatenate([jnp.pad(low, around), x, jnp.pad(high, around)], axis=dim)
        done.append(dim)
    return x


def from_everyone(x, axis):
    copies = jnp.broadcast_to(x, (lax.axis_size(axis), *x.shape))
    return lax.all_to_all(copies, axis, split_axis=0, concat_axis=0, tiled=True)


def over_copies(x, axis):
    everything = from_everyone(x, axis)
    return jnp.sum(everything, axis=0)


def together(arrays, axis):
    vector, at, outs = (jnp.concatenate([a.reshape(-1) for a in arrays]), 0, [])
    subtotal = over_copies(vector, axis)
    for a in arrays:
        outs.append(subtotal[at : at + a.size].reshape(a.shape))
        at += a.size
    return tuple(outs)


def of_everyone(x, axis):
    return from_everyone(x, axis).max(axis=0)


def box_three(padded, axis_pos):
    length_axis = padded.shape[axis_pos]
    lower_side = lax.slice_in_dim(padded, 0, length_axis - 2, axis=axis_pos)
    middle = lax.slice_in_dim(padded, 1, length_axis - 1, axis=axis_pos)
    upper_side = lax.slice_in_dim(padded, 2, length_axis, axis=axis_pos)
    return 0.25 * lower_side + 0.5 * middle + 0.25 * upper_side


def gradient_field(velocity_part, metric):
    around_span = with_halo(velocity_part, (("gz", 3),), 1, True)
    around_plane = with_halo_2(velocity_part, (("gx", 1), ("gy", 2)), 1)
    diff_chord = around_plane[:, 2:, 1:-1, :] - around_plane[:, :-2, 1:-1, :]
    diff_normal = around_plane[:, 1:-1, 2:, :] - around_plane[:, 1:-1, :-2, :]
    diff_span = around_span[:, :, :, 2:] - around_span[:, :, :, :-2]
    return jnp.stack(
        [0.5 * metric[0] * diff_chord, 0.5 * metric[1] * diff_normal, 0.5 * metric[2] * diff_span],
        axis=1,
    )


def strain_parts(gradients):
    strain = 0.5 * (gradients + jnp.swapaxes(gradients, 0, 1))
    magnitude = jnp.sqrt(2.0 * jnp.sum(strain * strain, axis=(0, 1)))
    strain_pairs = jnp.stack(
        [strain[row_index, col_index] for row_index, col_index in zip(pair_rows, pair_cols)]
    )
    return (strain_pairs, magnitude)


def make_fields(velocity_part, strain_pairs, magnitude):
    products = jnp.stack(
        [
            velocity_part[row_index] * velocity_part[col_index]
            for row_index, col_index in zip(pair_rows, pair_cols)
        ]
    )
    return jnp.concatenate([velocity_part, products, magnitude[None] * strain_pairs], axis=0)


def germano(filtered, strain_hat, magnitude_hat, delta_sq):
    numerator = jnp.zeros_like(delta_sq)
    denominator = jnp.zeros_like(delta_sq)
    for position in range(6):
        row_index = pair_rows[position]
        col_index = pair_cols[position]
        leonard = filtered[3 + position] - filtered[row_index] * filtered[col_index]
        model_term = (
            2.0
            * delta_sq
            * (filtered[9 + position] - ratio_square * magnitude_hat * strain_hat[position])
        )
        numerator = numerator + pair_weight[position] * leonard * model_term
        denominator = denominator + pair_weight[position] * model_term * model_term
    return (numerator, denominator)


def per_device(velocity, metric):
    delta_sq = (metric[0] * metric[1] * metric[2]) ** (-2.0 / 3.0)
    strain_pairs, magnitude = strain_parts(gradient_field(velocity, metric))
    fields = make_fields(velocity, strain_pairs, magnitude)
    span_done = box_three(with_halo(fields, (("gz", 3),), 1, True), 3)
    beside_all = with_halo(span_done, (("gx", 1), ("gy", 2)), 1, False)
    filtered = box_three(box_three(beside_all, 1), 2)
    strain_hat, magnitude_hat = strain_parts(gradient_field(filtered[0:3], metric))
    numerator, denominator = germano(filtered, strain_hat, magnitude_hat, delta_sq)
    span_cells = numerator.shape[2] * lax.axis_size("gz")
    num_part = jnp.sum(numerator, axis=2)
    den_part = jnp.sum(denominator, axis=2)
    line_num, line_den = together((num_part, den_part), "gz")
    line_coef = line_num / span_cells / (line_den / span_cells + eps_line)
    peak_coef = of_everyone(jnp.max(line_coef), ("gx", "gy"))
    coefficient = jnp.minimum(line_coef, 0.5 * peak_coef)
    viscosity = coefficient[:, :, None] * delta_sq * magnitude
    return (viscosity, coefficient)


def solution(mesh):
    return jax.shard_map(
        per_device,
        mesh=mesh,
        in_specs=(P(None, "gx", "gy", "gz"), P(None, "gx", "gy", "gz")),
        out_specs=(P("gx", "gy", "gz"), P("gx", "gy")),
        check_vma=False,
    )
```

profile of v0, /device:TPU:1, one launch (start us, length us, event | category | flops | bytes accessed | tf_op | source)
XLA Modules:
  0.0 150.9 jit_solution(697294129957950879)
XLA Ops:
  0.6 1.3 fusion.85
  1.9 6.0 %collective-permute-start.3 = (f32[3,16,1,256]{3,1,2,0:T(8,128)S(1)}, f32[3,16,1,256]{3,1,2,0:T(8,128)S(1)}, u32[]{:S(2)}, u32[]{:S(2)}) collective-permute-start(f32[3,16,1,256]{3,1,2,0:T(8,128)S(1)} %copy.122), channel_id=1, source_target_pairs={{0,4},{4,8},{8,12},{1,5},{5,9},{9,13},{2,6},{6,10},{10,14},{3,7},{... | collective-permute-start | bytes 147464 | tf_op jit(solution)/shard_map/ppermute | solution.py:36
  8.0 1.9 %collective-permute-start.2 = (f32[3,16,1,256]{3,1,2,0:T(8,128)S(1)}, f32[3,16,1,256]{3,1,2,0:T(8,128)S(1)}, u32[]{:S(2)}, u32[]{:S(2)}) collective-permute-start(f32[3,16,1,256]{3,1,2,0:T(8,128)S(1)} %copy.121), channel_id=1, source_target_pairs={{4,0},{8,4},{12,8},{5,1},{9,5},{13,9},{6,2},{10,6},{14,10},{7,3},{... | collective-permute-start | bytes 147464 | tf_op jit(solution)/shard_map/ppermute | solution.py:37
  9.9 0.8 fusion.86
  10.7 1.3 collective-permute-start
  12.0 4.0 %collective-permute-start.1 = (f32[3,1,16,256]{3,2,1,0:T(8,128)S(1)}, f32[3,1,16,256]{3,2,1,0:T(8,128)S(1)}, u32[]{:S(2)}, u32[]{:S(2)}) collective-permute-start(f32[3,1,16,256]{3,2,1,0:T(8,128)S(1)} %get-tuple-element.44), channel_id=1, source_target_pairs={{0,16},{16,32},{32,48},{48,64},{64,80},{80,96},{96,112},{112,128},... | collective-permute-start | bytes 147464 | tf_op jit(solution)/shard_map/ppermute | solution.py:36
  16.0 1.3 fusion.87
  17.3 2.8 %collective-permute-start.4 = (f32[3,16,16,1]{3,2,1,0:T(8,128)S(1)}, f32[3,16,16,1]{3,2,1,0:T(8,128)S(1)}, u32[]{:S(2)}, u32[]{:S(2)}) collective-permute-start(f32[3,16,16,1]{3,2,1,0:T(8,128)S(1)} %get-tuple-element.45), channel_id=1, source_target_pairs={{1,0},{2,1},{3,2},{0,3},{5,4},{6,5},{7,6},{4,7},{9,8},{10,9},{11,1... | collective-permute-start | bytes 9224 | tf_op jit(solution)/shard_map/ppermute | solution.py:23
  20.1 1.2 multiply_bitcast_fusion.2
  21.3 0.1 collective-permute-start.5
  21.6 5.8 %collective-permute-done.4 = f32[3,16,16,1]{3,2,1,0:T(8,128)S(1)} collective-permute-done((f32[3,16,16,1]{3,2,1,0:T(8,128)S(1)}, f32[3,16,16,1]{3,2,1,0:T(8,128)S(1)}, u32[]{:S(2)}, u32[]{:S(2)}) %collective-permute-start.4) | collective-permute-done | bytes 3104 | tf_op jit(solution)/shard_map/ppermute | solution.py:23
  27.4 3.9 %collective-permute-done.5 = f32[3,16,16,1]{3,2,1,0:T(8,128)S(1)} collective-permute-done((f32[3,16,16,1]{3,2,1,0:T(8,128)S(1)}, f32[3,16,16,1]{3,2,1,0:T(8,128)S(1)}, u32[]{:S(2)}, u32[]{:S(2)}) %collective-permute-start.5) | collective-permute-done | bytes 3104 | tf_op jit(solution)/shard_map/ppermute | solution.py:20
  31.3 0.8 fusion.28
  32.1 0.2 fusion.25
  32.4 0.2 pad_maximum_fusion.3
  32.6 0.4 multiply_reduce_fusion.1
  33.0 0.1 multiply_sqrt_fusion
  33.5 0.2 multiply_dynamic-update-slice_fusion
  33.7 1.9 %copy-done.1 = f32[15,16,16,256]{3,2,1,0:T(8,128)} copy-done((f32[15,16,16,256]{3,2,1,0:T(8,128)}, f32[15,16,16,256]{3,2,1,0:T(8,128)S(1)}, u32[]{:S(2)}) %copy-start.1) | copy-done | bytes 3932184
  35.5 2.0 %fusion.84 = (f32[15,16,16,1]{3,2,1,0:T(8,128)}, f32[15,16,16,1]{3,2,1,0:T(8,128)S(1)}) fusion(f32[15,16,16,256]{3,2,1,0:T(8,128)S(1)} %multiply_dynamic-update-slice_fusion), kind=kLoop, calls=%fused_computation.172 | loop fusion | bytes 61440 | tf_op jit(solution)/shard_map/slice | solution.py:21
  37.5 3.0 %copy.123 = f32[15,16,16,1]{2,1,3,0:T(8,128)S(1)} copy(f32[15,16,16,1]{3,2,1,0:T(8,128)} %get-tuple-element.25) | data formatting | bytes 30720
  40.5 0.1 collective-permute-start.6
  40.6 1.5 copy.124
  42.1 2.7 %collective-permute-start.7 = (f32[15,16,16,1]{2,1,3,0:T(8,128)S(1)}, f32[15,16,16,1]{2,1,3,0:T(8,128)S(1)}, u32[]{:S(2)}, u32[]{:S(2)}) collective-permute-start(f32[15,16,16,1]{2,1,3,0:T(8,128)S(1)} %copy.124), channel_id=1, source_target_pairs={{1,0},{2,1},{3,2},{0,3},{5,4},{6,5},{7,6},{4,7},{9,8},{10,9},{11,1... | collective-permute-start | bytes 46088 | tf_op jit(solution)/shard_map/ppermute | solution.py:23
  44.8 1.1 collective-permute-done.6
  45.9 1.5 copy.108
  47.3 2.8 %copy.110 = f32[15,16,16,1]{3,2,1,0:T(8,128)} copy(f32[15,16,16,1]{2,1,3,0:T(8,128)S(1)} %collective-permute-done.7) | data formatting | bytes 30720 | tf_op jit(solution)/shard_map/ppermute | solution.py:23
  50.1 6.6 %fusion.5 = f32[15,16,16,256]{3,2,1,0:T(8,128)S(1)} fusion(f32[15,16,16,1]{3,2,1,0:T(8,128)} %copy.110, f32[15,16,16,256]{3,2,1,0:T(8,128)} %copy-done.1, f32[15,16,16,1]{3,2,1,0:T(8,128)S(1)} %copy.108), kind=kLoop, calls=%fused_computation.13 | loop fusion | flops 6881280 | bytes 7895040 | tf_op jit(solution)/shard_map/add | solution.py:76
  56.8 4.8 %collective-permute-start.8 = (f32[15,1,16,256]{3,2,1,0:T(8,128)S(1)}, f32[15,1,16,256]{3,2,1,0:T(8,128)S(1)}, u32[]{:S(2)}, u32[]{:S(2)}) collective-permute-start(f32[15,1,16,256]{3,2,1,0:T(8,128)S(1)} %get-tuple-element.23), channel_id=1, source_target_pairs={{0,16},{16,32},{32,48},{48,64},{64,80},{80,96},{96,112},{112,128},... | collective-permute-start | bytes 737288 | tf_op jit(solution)/shard_map/ppermute | solution.py:20
  61.6 1.3 collective-permute-start.9
  62.9 8.9 %collective-permute-done.8 = f32[15,1,16,256]{3,2,1,0:T(8,128)S(1)} collective-permute-done((f32[15,1,16,256]{3,2,1,0:T(8,128)S(1)}, f32[15,1,16,256]{3,2,1,0:T(8,128)S(1)}, u32[]{:S(2)}, u32[]{:S(2)}) %collective-permute-start.8) | collective-permute-done | bytes 245792 | tf_op jit(solution)/shard_map/ppermute | solution.py:20
  71.8 0.4 pad_maximum_fusion.21
  72.2 3.0 %collective-permute-start.10 = (f32[15,18,1,256]{3,2,1,0:T(1,128)S(1)}, f32[15,18,1,256]{3,2,1,0:T(1,128)S(1)}, u32[]{:S(2)}, u32[]{:S(2)}) collective-permute-start(f32[15,18,1,256]{3,2,1,0:T(1,128)S(1)} %get-tuple-element.15), channel_id=1, source_target_pairs={{0,4},{4,8},{8,12},{1,5},{5,9},{9,13},{2,6},{6,10},{10,14},{3,7},{... | collective-permute-start | bytes 829448 | tf_op jit(solution)/shard_map/ppermute | solution.py:20
  75.2 2.1 %collective-permute-start.11 = (f32[15,18,1,256]{3,2,1,0:T(1,128)S(1)}, f32[15,18,1,256]{3,2,1,0:T(1,128)S(1)}, u32[]{:S(2)}, u32[]{:S(2)}) collective-permute-start(f32[15,18,1,256]{3,2,1,0:T(1,128)S(1)} %get-tuple-element.16), channel_id=1, source_target_pairs={{4,0},{8,4},{12,8},{5,1},{9,5},{13,9},{6,2},{10,6},{14,10},{7,3},{... | collective-permute-start | bytes 829448 | tf_op jit(solution)/shard_map/ppermute | solution.py:23
  77.3 1.3 collective-permute-done.10
  78.6 5.9 %collective-permute-done.11 = f32[15,18,1,256]{3,2,1,0:T(1,128)S(1)} collective-permute-done((f32[15,18,1,256]{3,2,1,0:T(1,128)S(1)}, f32[15,18,1,256]{3,2,1,0:T(1,128)S(1)}, u32[]{:S(2)}, u32[]{:S(2)}) %collective-permute-start.11) | collective-permute-done | bytes 276512 | tf_op jit(solution)/shard_map/ppermute | solution.py:23
  84.5 1.4 pad_maximum_fusion
  85.9 1.7 %fusion = f32[15,16,18,256]{3,2,1,0:T(8,128)S(1)} fusion(f32[15,18,18,256]{3,2,1,0:T(8,128)S(1)} %pad_maximum_fusion), kind=kLoop, calls=%fused_computation.2 | loop fusion | flops 5529600 | bytes 17694720 | tf_op jit(solution)/shard_map/add | solution.py:76
  87.6 1.2 fusion.2
  88.8 0.1 fusion.80
  88.9 1.9 %collective-permute-start.15 = (f32[3,16,1,256]{3,1,2,0:T(8,128)S(1)}, f32[3,16,1,256]{3,1,2,0:T(8,128)S(1)}, u32[]{:S(2)}, u32[]{:S(2)}) collective-permute-start(f32[3,16,1,256]{3,1,2,0:T(8,128)S(1)} %copy.113), channel_id=1, source_target_pairs={{0,4},{4,8},{8,12},{1,5},{5,9},{9,13},{2,6},{6,10},{10,14},{3,7},{... | collective-permute-start | bytes 147464 | tf_op jit(solution)/shard_map/ppermute | solution.py:36
  90.8 2.4 %collective-permute-start.14 = (f32[3,16,1,256]{3,1,2,0:T(8,128)S(1)}, f32[3,16,1,256]{3,1,2,0:T(8,128)S(1)}, u32[]{:S(2)}, u32[]{:S(2)}) collective-permute-start(f32[3,16,1,256]{3,1,2,0:T(8,128)S(1)} %copy.111), channel_id=1, source_target_pairs={{4,0},{8,4},{12,8},{5,1},{9,5},{13,9},{6,2},{10,6},{14,10},{7,3},{... | collective-permute-start | bytes 147464 | tf_op jit(solution)/shard_map/ppermute | solution.py:37
  93.3 3.2 %collective-permute-start.13 = (f32[3,1,16,256]{3,2,1,0:T(8,128)S(1)}, f32[3,1,16,256]{3,2,1,0:T(8,128)S(1)}, u32[]{:S(2)}, u32[]{:S(2)}) collective-permute-start(f32[3,1,16,256]{3,2,1,0:T(8,128)S(1)} %get-tuple-element.19), channel_id=1, source_target_pairs={{0,16},{16,32},{32,48},{48,64},{64,80},{80,96},{96,112},{112,128},... | collective-permute-start | bytes 147464 | tf_op jit(solution)/shard_map/ppermute | solution.py:36
  96.5 1.3 collective-permute-start.12
  97.8 0.2 fusion.82
  97.9 3.1 %collective-permute-start.16 = (f32[3,16,16,1]{3,2,1,0:T(8,128)S(1)}, f32[3,16,16,1]{3,2,1,0:T(8,128)S(1)}, u32[]{:S(2)}, u32[]{:S(2)}) collective-permute-start(f32[3,16,16,1]{3,2,1,0:T(8,128)S(1)} %get-tuple-element.21), channel_id=1, source_target_pairs={{1,0},{2,1},{3,2},{0,3},{5,4},{6,5},{7,6},{4,7},{9,8},{10,9},{11,1... | collective-permute-start | bytes 9224 | tf_op jit(solution)/shard_map/ppermute | solution.py:23
  101.2 8.6 %collective-permute-done.16 = f32[3,16,16,1]{3,2,1,0:T(8,128)S(1)} collective-permute-done((f32[3,16,16,1]{3,2,1,0:T(8,128)S(1)}, f32[3,16,16,1]{3,2,1,0:T(8,128)S(1)}, u32[]{:S(2)}, u32[]{:S(2)}) %collective-permute-start.16) | collective-permute-done | bytes 3104 | tf_op jit(solution)/shard_map/ppermute | solution.py:23
  109.8 3.1 %collective-permute-done.17 = f32[3,16,16,1]{3,2,1,0:T(8,128)S(1)} collective-permute-done((f32[3,16,16,1]{3,2,1,0:T(8,128)S(1)}, f32[3,16,16,1]{3,2,1,0:T(8,128)S(1)}, u32[]{:S(2)}, u32[]{:S(2)}) %collective-permute-start.17) | collective-permute-done | bytes 3104 | tf_op jit(solution)/shard_map/ppermute | solution.py:20
  113.0 0.8 fusion.19
  113.8 0.2 pad_maximum_fusion.4
  114.1 0.5 multiply_reduce_fusion
  114.6 0.4 copy-done.2
  114.9 0.4 fusion.69
  115.4 0.4 fusion.63
  115.7 0.4 fusion.40
  116.2 0.1 reshape.88
  116.2 0.1 reshape.89
  116.4 6.5 %all_to_all.12 = f32[4,1,512]{2,1,0:T(1,128)S(1)} all-to-all(f32[4,1,512]{2,1,0:T(1,128)S(1)} %broadcast_in_dim.4), channel_id=1, replica_groups=mesh['gx'=16,'gy'=4,'gz'=4] {'gz'}, dimensions={0} | all-to-all | bytes 16384 | tf_op jit(solution)/shard_map/all_to_all | solution.py:50
  122.9 0.6 fusion.79
  123.5 0.7 broadcast_in_dim.5
  124.2 24.5 %all_to_all.13 = f32[64,1,1]{2,1,0:T(1,128)S(1)} all-to-all(f32[64,1,1]{2,1,0:T(1,128)S(1)} %broadcast_in_dim.5), channel_id=1, replica_groups=mesh['gx'=16,'gy'=4,'gz'=4] {'gx','gy'}, dimensions={0} | all-to-all | bytes 512 | tf_op jit(solution)/shard_map/all_to_all | solution.py:50
  148.7 0.7 reduce_max.19
  150.0 0.1 min.15
  150.1 0.9 fusion.78
  (46 shorter events, 0.7 us)
Async XLA Ops:
  0.6 30.7 %copy-start = (f32[3,16,16,256]{3,2,1,0:T(8,128)S(1)}, f32[3,16,16,256]{3,2,1,0:T(8,128)}, u32[]{:S(2)}) copy-start(f32[3,16,16,256]{3,2,1,0:T(8,128)} %param.2) | copy-start | bytes 2359300
  1.9 19.5 %collective-permute-start.3 = (f32[3,16,1,256]{3,1,2,0:T(8,128)S(1)}, f32[3,16,1,256]{3,1,2,0:T(8,128)S(1)}, u32[]{:S(2)}, u32[]{:S(2)}) collective-permute-start(f32[3,16,1,256]{3,1,2,0:T(8,128)S(1)} %copy.122), channel_id=1, source_target_pairs={{0,4},{4,8},{8,12},{1,5},{5,9},{9,13},{2,6},{6,10},{10,14},{3,7},{... | collective-permute-start | bytes 147464 | tf_op jit(solution)/shard_map/ppermute | solution.py:36
  8.0 13.5 %collective-permute-start.2 = (f32[3,16,1,256]{3,1,2,0:T(8,128)S(1)}, f32[3,16,1,256]{3,1,2,0:T(8,128)S(1)}, u32[]{:S(2)}, u32[]{:S(2)}) collective-permute-start(f32[3,16,1,256]{3,1,2,0:T(8,128)S(1)} %copy.121), channel_id=1, source_target_pairs={{4,0},{8,4},{12,8},{5,1},{9,5},{13,9},{6,2},{10,6},{14,10},{7,3},{... | collective-permute-start | bytes 147464 | tf_op jit(solution)/shard_map/ppermute | solution.py:37
  10.7 20.6 %collective-permute-start = (f32[3,1,16,256]{3,2,1,0:T(8,128)S(1)}, f32[3,1,16,256]{3,2,1,0:T(8,128)S(1)}, u32[]{:S(2)}, u32[]{:S(2)}) collective-permute-start(f32[3,1,16,256]{3,2,1,0:T(8,128)S(1)} %get-tuple-element.43), channel_id=1, source_target_pairs={{16,0},{32,16},{48,32},{64,48},{80,64},{96,80},{112,96},{128,112},... | collective-permute-start | bytes 147464 | tf_op jit(solution)/shard_map/ppermute | solution.py:37
  12.0 9.3 %collective-permute-start.1 = (f32[3,1,16,256]{3,2,1,0:T(8,128)S(1)}, f32[3,1,16,256]{3,2,1,0:T(8,128)S(1)}, u32[]{:S(2)}, u32[]{:S(2)}) collective-permute-start(f32[3,1,16,256]{3,2,1,0:T(8,128)S(1)} %get-tuple-element.44), channel_id=1, source_target_pairs={{0,16},{16,32},{32,48},{48,64},{64,80},{80,96},{96,112},{112,128},... | collective-permute-start | bytes 147464 | tf_op jit(solution)/shard_map/ppermute | solution.py:36
  17.3 10.1 %collective-permute-start.4 = (f32[3,16,16,1]{3,2,1,0:T(8,128)S(1)}, f32[3,16,16,1]{3,2,1,0:T(8,128)S(1)}, u32[]{:S(2)}, u32[]{:S(2)}) collective-permute-start(f32[3,16,16,1]{3,2,1,0:T(8,128)S(1)} %get-tuple-element.45), channel_id=1, source_target_pairs={{1,0},{2,1},{3,2},{0,3},{5,4},{6,5},{7,6},{4,7},{9,8},{10,9},{11,1... | collective-permute-start | bytes 9224 | tf_op jit(solution)/shard_map/ppermute | solution.py:23
  21.3 10.0 %collective-permute-start.5 = (f32[3,16,16,1]{3,2,1,0:T(8,128)S(1)}, f32[3,16,16,1]{3,2,1,0:T(8,128)S(1)}, u32[]{:S(2)}, u32[]{:S(2)}) collective-permute-start(f32[3,16,16,1]{3,2,1,0:T(8,128)S(1)} %get-tuple-element.46), channel_id=1, source_target_pairs={{0,1},{1,2},{2,3},{3,0},{4,5},{5,6},{6,7},{7,4},{8,9},{9,10},{10,1... | collective-permute-start | bytes 9224 | tf_op jit(solution)/shard_map/ppermute | solution.py:20
  33.7 1.9 %copy-start.1 = (f32[15,16,16,256]{3,2,1,0:T(8,128)}, f32[15,16,16,256]{3,2,1,0:T(8,128)S(1)}, u32[]{:S(2)}) copy-start(f32[15,16,16,256]{3,2,1,0:T(8,128)S(1)} %multiply_dynamic-update-slice_fusion) | copy-start | bytes 11796484
  40.5 5.3 %collective-permute-start.6 = (f32[15,16,16,1]{2,1,3,0:T(8,128)S(1)}, f32[15,16,16,1]{2,1,3,0:T(8,128)S(1)}, u32[]{:S(2)}, u32[]{:S(2)}) collective-permute-start(f32[15,16,16,1]{2,1,3,0:T(8,128)S(1)} %copy.123), channel_id=1, source_target_pairs={{0,1},{1,2},{2,3},{3,0},{4,5},{5,6},{6,7},{7,4},{8,9},{9,10},{10,1... | collective-permute-start | bytes 46088 | tf_op jit(solution)/shard_map/ppermute | solution.py:20
  42.1 5.3 %collective-permute-start.7 = (f32[15,16,16,1]{2,1,3,0:T(8,128)S(1)}, f32[15,16,16,1]{2,1,3,0:T(8,128)S(1)}, u32[]{:S(2)}, u32[]{:S(2)}) collective-permute-start(f32[15,16,16,1]{2,1,3,0:T(8,128)S(1)} %copy.124), channel_id=1, source_target_pairs={{1,0},{2,1},{3,2},{0,3},{5,4},{6,5},{7,6},{4,7},{9,8},{10,9},{11,1... | collective-permute-start | bytes 46088 | tf_op jit(solution)/shard_map/ppermute | solution.py:23
  56.8 15.0 %collective-permute-start.8 = (f32[15,1,16,256]{3,2,1,0:T(8,128)S(1)}, f32[15,1,16,256]{3,2,1,0:T(8,128)S(1)}, u32[]{:S(2)}, u32[]{:S(2)}) collective-permute-start(f32[15,1,16,256]{3,2,1,0:T(8,128)S(1)} %get-tuple-element.23), channel_id=1, source_target_pairs={{0,16},{16,32},{32,48},{48,64},{64,80},{80,96},{96,112},{112,128},... | collective-permute-start | bytes 737288 | tf_op jit(solution)/shard_map/ppermute | solution.py:20
  61.6 10.2 %collective-permute-start.9 = (f32[15,1,16,256]{3,2,1,0:T(8,128)S(1)}, f32[15,1,16,256]{3,2,1,0:T(8,128)S(1)}, u32[]{:S(2)}, u32[]{:S(2)}) collective-permute-start(f32[15,1,16,256]{3,2,1,0:T(8,128)S(1)} %get-tuple-element.24), channel_id=1, source_target_pairs={{16,0},{32,16},{48,32},{64,48},{80,64},{96,80},{112,96},{128,112},... | collective-permute-start | bytes 737288 | tf_op jit(solution)/shard_map/ppermute | solution.py:23
  72.2 6.4 %collective-permute-start.10 = (f32[15,18,1,256]{3,2,1,0:T(1,128)S(1)}, f32[15,18,1,256]{3,2,1,0:T(1,128)S(1)}, u32[]{:S(2)}, u32[]{:S(2)}) collective-permute-start(f32[15,18,1,256]{3,2,1,0:T(1,128)S(1)} %get-tuple-element.15), channel_id=1, source_target_pairs={{0,4},{4,8},{8,12},{1,5},{5,9},{9,13},{2,6},{6,10},{10,14},{3,7},{... | collective-permute-start | bytes 829448 | tf_op jit(solution)/shard_map/ppermute | solution.py:20
  75.2 9.3 %collective-permute-start.11 = (f32[15,18,1,256]{3,2,1,0:T(1,128)S(1)}, f32[15,18,1,256]{3,2,1,0:T(1,128)S(1)}, u32[]{:S(2)}, u32[]{:S(2)}) collective-permute-start(f32[15,18,1,256]{3,2,1,0:T(1,128)S(1)} %get-tuple-element.16), channel_id=1, source_target_pairs={{4,0},{8,4},{12,8},{5,1},{9,5},{13,9},{6,2},{10,6},{14,10},{7,3},{... | collective-permute-start | bytes 829448 | tf_op jit(solution)/shard_map/ppermute | solution.py:23
  88.9 12.1 %collective-permute-start.15 = (f32[3,16,1,256]{3,1,2,0:T(8,128)S(1)}, f32[3,16,1,256]{3,1,2,0:T(8,128)S(1)}, u32[]{:S(2)}, u32[]{:S(2)}) collective-permute-start(f32[3,16,1,256]{3,1,2,0:T(8,128)S(1)} %copy.113), channel_id=1, source_target_pairs={{0,4},{4,8},{8,12},{1,5},{5,9},{9,13},{2,6},{6,10},{10,14},{3,7},{... | collective-permute-start | bytes 147464 | tf_op jit(solution)/shard_map/ppermute | solution.py:36
  90.8 10.3 %collective-permute-start.14 = (f32[3,16,1,256]{3,1,2,0:T(8,128)S(1)}, f32[3,16,1,256]{3,1,2,0:T(8,128)S(1)}, u32[]{:S(2)}, u32[]{:S(2)}) collective-permute-start(f32[3,16,1,256]{3,1,2,0:T(8,128)S(1)} %copy.111), channel_id=1, source_target_pairs={{4,0},{8,4},{12,8},{5,1},{9,5},{13,9},{6,2},{10,6},{14,10},{7,3},{... | collective-permute-start | bytes 147464 | tf_op jit(solution)/shard_map/ppermute | solution.py:37
  93.3 19.7 %collective-permute-start.13 = (f32[3,1,16,256]{3,2,1,0:T(8,128)S(1)}, f32[3,1,16,256]{3,2,1,0:T(8,128)S(1)}, u32[]{:S(2)}, u32[]{:S(2)}) collective-permute-start(f32[3,1,16,256]{3,2,1,0:T(8,128)S(1)} %get-tuple-element.19), channel_id=1, source_target_pairs={{0,16},{16,32},{32,48},{48,64},{64,80},{80,96},{96,112},{112,128},... | collective-permute-start | bytes 147464 | tf_op jit(solution)/shard_map/ppermute | solution.py:36
  96.5 16.5 %collective-permute-start.12 = (f32[3,1,16,256]{3,2,1,0:T(8,128)S(1)}, f32[3,1,16,256]{3,2,1,0:T(8,128)S(1)}, u32[]{:S(2)}, u32[]{:S(2)}) collective-permute-start(f32[3,1,16,256]{3,2,1,0:T(8,128)S(1)} %get-tuple-element.20), channel_id=1, source_target_pairs={{16,0},{32,16},{48,32},{64,48},{80,64},{96,80},{112,96},{128,112},... | collective-permute-start | bytes 147464 | tf_op jit(solution)/shard_map/ppermute | solution.py:37
  97.9 11.9 %collective-permute-start.16 = (f32[3,16,16,1]{3,2,1,0:T(8,128)S(1)}, f32[3,16,16,1]{3,2,1,0:T(8,128)S(1)}, u32[]{:S(2)}, u32[]{:S(2)}) collective-permute-start(f32[3,16,16,1]{3,2,1,0:T(8,128)S(1)} %get-tuple-element.21), channel_id=1, source_target_pairs={{1,0},{2,1},{3,2},{0,3},{5,4},{6,5},{7,6},{4,7},{9,8},{10,9},{11,1... | collective-permute-start | bytes 9224 | tf_op jit(solution)/shard_map/ppermute | solution.py:23
  101.0 11.9 %collective-permute-start.17 = (f32[3,16,16,1]{3,2,1,0:T(8,128)S(1)}, f32[3,16,16,1]{3,2,1,0:T(8,128)S(1)}, u32[]{:S(2)}, u32[]{:S(2)}) collective-permute-start(f32[3,16,16,1]{3,2,1,0:T(8,128)S(1)} %get-tuple-element.22), channel_id=1, source_target_pairs={{0,1},{1,2},{2,3},{3,0},{4,5},{5,6},{6,7},{7,4},{8,9},{9,10},{10,1... | collective-permute-start | bytes 9224 | tf_op jit(solution)/shard_map/ppermute | solution.py:20
  113.8 1.1 copy-start.2
  150.1 0.9 copy-start.3
where the time goes:
time: 152 us; the launch traced here: 151 us
  starting transfers between devices  42 us (28%)
  waiting for transfers between devices  38.7 us (25%)
  blocking collectives  31 us (20%)
  other arithmetic  19.5 us (13%)
  local copies, waits for them, and re-layouts  17.9 us (12%)
  between operations  1.82 us (1%)
    all_to_all x2, blocking collectives, from_everyone(): return lax.all_to_all(copies, axis, split_axis=0, concat_axis=0, tiled=True)  31 us
    ppermute x5, waiting for transfers between devices, with_halo(): lax.ppermute(lax.slice_in_dim(block, 0, width, axis=dim), axis, backward)  20.3 us
    ppermute x5, waiting for transfers between devices, with_halo(): lax.ppermute(lax.slice_in_dim(block, block.shape[dim] - width, None, axis...  18.4 us
    ppermute x4, starting transfers between devices, with_halo_2(): lax.ppermute(last, axis, up)  15.1 us
    ppermute x5, starting transfers between devices, with_halo(): lax.ppermute(lax.slice_in_dim(block, 0, width, axis=dim), axis, backward)  12 us
    add x3, other arithmetic, box_three(): return 0.25 * lower_side + 0.5 * middle + 0.25 * upper_side  9.52 us
    ppermute x5, starting transfers between devices, with_halo(): lax.ppermute(lax.slice_in_dim(block, block.shape[dim] - width, None, axis...  7.97 us
    unnamed x20, local copies, waits for them, and re-layouts  6.94 us
  transfers between devices with their start and end apart: 18, of which 8 were waited for; matrix products, arithmetic and copies ran while one was open for 4% of the time, Pallas kernels for 0%

commit v1 on v0

v1 whole, which is shorter than its diff:
```python
import functools
import jax
import jax.numpy as jnp
from jax import lax
from jax.experimental import pallas as pl
from jax.experimental.pallas import tpu as pltpu
from jax.sharding import PartitionSpec as P

PAIRS = ((0, 0), (1, 1), (2, 2), (0, 1), (0, 2), (1, 2))
F32 = jnp.float32
MESH = pl.DeviceIdType.MESH
PITCH = 32
BASE = 8


def strain_of(diffs, m):
    g = [[m[j] * diffs[i][j] for j in range(3)] for i in range(3)]
    s = [g[a][a] if a == b else g[a][b] + g[b][a] for a, b in PAIRS]
    diag = s[0] * s[0] + s[1] * s[1] + s[2] * s[2]
    off = s[3] * s[3] + s[4] * s[4] + s[5] * s[5]
    return s, jnp.sqrt(0.5 * diag + 0.25 * off)


def kernel(sizes, vel, met, visc, coef_out, U, O6, SY, RY, SC, RC, RO, ZG, SZX, RZX, SZY, RZY,
           RZC, TZ, UE, ZE, VE, VHE, T, YF, YV, VH, MB, DM, LN, RX, RZ, PK, lsem, ssem, rsem):
    ngx, ngy, ngz = sizes
    nx = vel.shape[1]
    ny = vel.shape[2]
    nz = vel.shape[3]
    gx, gy, gz = lax.axis_index("gx"), lax.axis_index("gy"), lax.axis_index("gz")
    nzc = ngx // 2
    xlo, xz = lax.rem(gx, 2), lax.div(gx, 2)
    has = {("x", 0): gx > 0, ("x", 1): gx < ngx - 1, ("y", 0): gy > 0, ("y", 1): gy < ngy - 1}

    ins = []
    for zt in range(2):
        for k, ref in enumerate((vel, met)):
            cp = pltpu.make_async_copy(
                ref.at[:, :, :, pl.ds(128 * zt, 128)],
                U.at[pl.ds(3 * k, 3), zt, pl.ds(2, nx), pl.ds(BASE, ny), :],
                lsem.at[2 * zt + k],
            )
            cp.start()
            ins.append(cp)

    z8 = jnp.zeros((8, 128), F32)
    for f in range(6):
        for zt in range(2):
            for X in (0, 1, nx + 2, nx + 3):
                for r in range(0, ny, 8):
                    U[f, zt, X, BASE + r : BASE + r + 8, :] = z8
    RY[...] = jnp.zeros(RY.shape, F32)
    RC[...] = jnp.zeros(RC.shape, F32)
    RZX[...] = jnp.zeros(RZX.shape, F32)
    RZY[...] = jnp.zeros(RZY.shape, F32)
    RZC[...] = jnp.zeros(RZC.shape, F32)

    bar = pltpu.get_barrier_semaphore()

    def greet(dev):
        pl.semaphore_signal(bar, inc=1, device_id=dev, device_id_type=MESH)

    def dx(s):
        return gx + (1 if s else -1)

    def dy(s):
        return gy + (1 if s else -1)

    for k in range(1, ngz):
        greet({"gz": lax.rem(gz + k, ngz)})
    for s in range(2):
        @pl.when(has["x", s])
        def _():
            greet({"gx": dx(s)})

        @pl.when(has["y", s])
        def _():
            greet({"gy": dy(s)})

        for q in range(2):
            @pl.when(jnp.logical_and(has["x", s], has["y", q]))
            def _():
                greet({"gx": dx(s), "gy": dy(q)})

    nxc = 2 * ngy
    me_c = xlo * ngy + gy

    def xc_dev(k):
        c = lax.rem(me_c + k, nxc)
        return c, {"gx": xz * 2 + lax.div(c, ngy), "gy": lax.rem(c, ngy)}

    def z_dev(k):
        c = lax.rem(xz + k, nzc)
        return c, {"gx": c * 2 + xlo}

    for k in range(1, nxc):
        greet(xc_dev(k)[1])
    for k in range(1, nzc):
        greet(z_dev(k)[1])
    ex = has["x", 0].astype(jnp.int32) + has["x", 1].astype(jnp.int32)
    ey = has["y", 0].astype(jnp.int32) + has["y", 1].astype(jnp.int32)

    lane = lax.broadcasted_iota(jnp.int32, (8, 128), 1)
    lx = lax.shift_right_logical(lane * 43, 8)
    lc = lane - 6 * lx
    row = lax.broadcasted_iota(jnp.int32, (8, 128), 0)
    for cp in ins:
        cp.wait()
    half = lane < 64
    for f in range(6):
        for t in range(2):
            acc = z8
            rows = slice(BASE + 8 * t, BASE + 8 * t + 8)
            for X in range(2, nx + 2):
                a = jnp.where(half, U[f, 0, X, rows, :], U[f, 1, X, rows, :])
                acc = jnp.where(lx == X, pltpu.roll(a, (6 * X + 2) % 128, 1), acc)
            O6[f, 8 * t : 8 * t + 8, :] = acc

    for s in range(2):
        for f in range(6):
            for k in range(2):
                if f >= 3 and k != s:
                    continue
                y = (ny - 2 + k) if s else k
                slab = 2 * f + k if f < 3 else 3 + f
                for zt in range(2):
                    SY[s, slab, zt, :, :] = U[f, zt, pl.ds(2, nx), BASE + y, :]

    def corner_rows(out, sx, sy):
        r = 0
        for f in range(6):
            for kx in range(2):
                for ky in range(2):
                    if f >= 3 and (kx != sx or ky != sy):
                        continue
                    if out:
                        X = (nx if sx else 2) + kx
                        y = (ny - 2 if sy else 0) + ky
                    else:
                        X = (nx + 2 if sx else 0) + kx
                        y = (ny if sy else -2) + ky
                    yield r, f, X, y + BASE
                    r += 1

    for sx in range(2):
        for sy in range(2):
            for r, f, X, yr in corner_rows(True, sx, sy):
                for zt in range(2):
                    SC[2 * sx + sy, zt, r : r + 1, :] = U[f, zt, X, yr : yr + 1, :]

    pl.semaphore_wait(bar, (ngz - 1) + (nxc - 1) + (nzc - 1) + ex + ey + ex * ey)

    waits_send, waits_recv = [], {}

    def put(n, src, dst, dev, send_if=None, recv_if=None):
        cp = pltpu.make_async_remote_copy(
            src_ref=src, dst_ref=dst, send_sem=ssem.at[n], recv_sem=rsem.at[n],
            device_id=dev, device_id_type=MESH)
        if send_if is None:
            cp.start()
        else:
            pl.when(send_if)(cp.start)
        waits_send.append((cp, send_if))
        waits_recv[n] = (cp, recv_if)

    def got(n):
        cp, cond = waits_recv[n]
        if cond is None:
            cp.wait_recv()
        else:
            pl.when(cond)(cp.wait_recv)

    for s in range(2):
        put(s, O6, RO.at[1 - s], {"gz": lax.rem(gz + (1 if s else ngz - 1), ngz)})
    for s in range(2):
        put(2 + s, SY.at[s], RY.at[1 - s], {"gy": dy(s)}, has["y", s], has["y", 1 - s])
    for sx in range(2):
        for sy in range(2):
            c, o = 2 * sx + sy, 2 * (1 - sx) + 1 - sy
            put(8 + c, SC.at[c], RC.at[o], {"gx": dx(sx), "gy": dy(sy)},
                jnp.logical_and(has["x", sx], has["y", sy]),
                jnp.logical_and(has["x", 1 - sx], has["y", 1 - sy]))
    rr = pl.ds(BASE, ny)
    for s in range(2):
        far, near = (nx, nx + 1) if s else (3, 2)
        gfar, gnear = (0, 1) if s else (nx + 3, nx + 2)
        put(4 + s, U.at[:, :, near, rr, :], U.at[:, :, gnear, rr, :], {"gx": dx(s)},
            has["x", s], has["x", 1 - s])
        put(6 + s, U.at[pl.ds(0, 3), :, far, rr, :], U.at[pl.ds(0, 3), :, gfar, rr, :],
            {"gx": dx(s)}, has["x", s], has["x", 1 - s])

    got(0)
    got(1)
    lanes_x = jnp.logical_and(lx >= 2, lx < nx + 2)
    for f in range(6):
        ZG[f, 0:8, :] = z8
        ZG[f, 24:32, :] = z8
        for t in range(2):
            rows = slice(8 * t, 8 * t + 8)
            own = O6[f, rows, :]
            right = pltpu.roll(jnp.where(lc == 1, own, RO[1, f, rows, :]), 2, 1)
            z = jnp.where(lc < 2, RO[0, f, rows, :], jnp.where(lc == 2, own, right))
            ZG[f, BASE + 8 * t : BASE + 8 * t + 8, :] = jnp.where(lanes_x, z, 0.0)
    for s in range(2):
        first = 6 * (nx if s else 2)
        for t in range(2):
            acc = z8
            for f in range(6):
                part = pltpu.roll(ZG[f, BASE + 8 * t : BASE + 8 * t + 8, :], (12 * f - first) % 128, 1)
                acc = jnp.where(jnp.logical_and(lane >= 12 * f, lane < 12 * f + 12), part, acc)
            SZX[s, 8 * t : 8 * t + 8, :] = acc
        y = ny - 2 if s else 0
        for f in range(6):
            SZY[s, 2 * f : 2 * f + 2, :] = ZG[f, BASE + y : BASE + y + 2, :]
    for s in range(2):
        put(14 + s, SZY.at[s], RZY.at[1 - s], {"gy": dy(s)}, has["y", s], has["y", 1 - s])
        put(12 + s, SZX.at[s], RZX.at[1 - s], {"gx": dx(s)}, has["x", s], has["x", 1 - s])
    for sx in range(2):
        for sy in range(2):
            c, o = 2 * sx + sy, 2 * (1 - sx) + 1 - sy
            put(16 + c, SZX.at[sx, pl.ds(ny - 8 if sy else 0, 8), :], RZC.at[o],
                {"gx": dx(sx), "gy": dy(sy)},
                jnp.logical_and(has["x", sx], has["y", sy]),
                jnp.logical_and(has["x", 1 - sx], has["y", 1 - sy]))

    for n in range(2, 20):
        got(n)

    for s in range(2):
        for f in range(6):
            for k in range(2):
                if f >= 3 and k == s:
                    continue
                y = (ny + k) if s else k - 2
                slab = 2 * f + k if f < 3 else 3 + f
                for zt in range(2):
                    U[f, zt, pl.ds(2, nx), BASE + y, :] = RY[s, slab, zt, :, :]
    for sx in range(2):
        for sy in range(2):
            src = {}
            r = 0
            for f in range(6):
                for kx in range(2):
                    for ky in range(2):
                        if f >= 3 and (kx != 1 - sx or ky != 1 - sy):
                            continue
                        src[f, kx, ky] = r
                        r += 1
            for (f, kx, ky), r in src.items():
                X = (nx + 2 if sx else 0) + kx
                yr = (ny if sy else -2) + ky + BASE
                for zt in range(2):
                    U[f, zt, X, yr : yr + 1, :] = RC[2 * sx + sy, zt, r : r + 1, :]
    for f in range(6):
        for t in range(2):
            rows = slice(BASE + 8 * t, BASE + 8 * t + 8)
            z = ZG[f, rows, :]
            for s in range(2):
                at = 6 * (nx + 2) if s else 0
                part = pltpu.roll(RZX[s, 8 * t : 8 * t + 8, :], (at - 12 * f) % 128, 1)
                z = jnp.where(jnp.logical_and(lane >= at, lane < at + 12), part, z)
            ZG[f, rows, :] = z
        for sy in range(2):
            yr = BASE + (ny if sy else -2)
            z = RZY[sy, 2 * f : 2 * f + 2, :]
            for sx in range(2):
                at = 6 * (nx + 2) if sx else 0
                tile = RZC[2 * sx + sy]
                part = pltpu.roll(tile, (at - 12 * f) % 128, 1)
                part = part[0:2] if sy else part[6:8]
                lane2 = lane[0:2]
                z = jnp.where(jnp.logical_and(lane2 >= at, lane2 < at + 12), part, z)
            ZG[f, yr : yr + 2, :] = z

    def edge(a):
        return jnp.where(lc == 0, pltpu.roll(a, 124, 1), a)

    def xsum(a):
        return pltpu.roll(a, 6, 1) + 2.0 * a + pltpu.roll(a, 122, 1)

    xd = lambda a: pltpu.roll(a, 122, 1) - pltpu.roll(a, 6, 1)
    zd = lambda a: pltpu.roll(a, 127, 1) - pltpu.roll(a, 1, 1)
    for t in range(3):
        r0 = BASE - 1 + 8 * t
        at = lambda f, d: ZG[f, r0 + d : r0 + d + 8, :]
        u = [at(i, 0) for i in range(3)]
        up = [at(i, 1) for i in range(3)]
        dn = [at(i, -1) for i in range(3)]
        m = [at(3 + j, 0) for j in range(3)]
        d = [[xd(u[i]), up[i] - dn[i], zd(u[i])] for i in range(3)]
        s, mag = strain_of(d, m)
        for p, (a, b) in enumerate(PAIRS):
            TZ[p, 8 * t : 8 * t + 8, :] = u[a] * u[b]
            TZ[6 + p, 8 * t : 8 * t + 8, :] = (0.5 if a == b else 0.25) * mag * s[p]
        for i in range(3):
            UE[i, 8 * t : 8 * t + 8, :] = edge(u[i])
            v = xsum(up[i] + dn[i] + 2.0 * u[i])
            VE[i, 8 * t : 8 * t + 8, :] = edge(v)
            vz = (1.0 / 64.0) * (pltpu.roll(v, 1, 1) + 2.0 * v + pltpu.roll(v, 127, 1))
            VHE[i, 8 * t : 8 * t + 8, :] = edge(vz)
    for p in range(12):
        for t in range(2):
            a = TZ[p, 8 * t : 8 * t + 8, :] + 2.0 * TZ[p, 8 * t + 1 : 8 * t + 9, :] + TZ[p, 8 * t + 2 : 8 * t + 10, :]
            ZE[p, 8 * t : 8 * t + 8, :] = edge(xsum(a))

    first_lane, last_lane = lane == 0, lane == 127

    def zshift(a, e):
        p0, p1 = pltpu.roll(a[0], 1, 1), pltpu.roll(a[1], 1, 1)
        n0, n1 = pltpu.roll(a[0], 127, 1), pltpu.roll(a[1], 127, 1)
        prev = (jnp.where(first_lane, e, p0), jnp.where(first_lane, p0, p1))
        nxt = (jnp.where(last_lane, n1, n0), jnp.where(last_lane, e, n1))
        return prev, nxt

    def stage_a(X, _):
        turn = 127 - 6 * X
        for t in range(3):
            r0 = BASE - 1 + 8 * t
            u = [[U[i, zt, X, r0 : r0 + 8, :] for zt in range(2)] for i in range(3)]
            zs = [zshift(u[i], pltpu.roll(UE[i, 8 * t : 8 * t + 8, :], turn, 1)) for i in range(3)]
            for zt in range(2):
                d = []
                for i in range(3):
                    ddx = U[i, zt, X + 1, r0 : r0 + 8, :] - U[i, zt, X - 1, r0 : r0 + 8, :]
                    ddy = U[i, zt, X, r0 + 1 : r0 + 9, :] - U[i, zt, X, r0 - 1 : r0 + 7, :]
                    d.append([ddx, ddy, zs[i][1][zt] - zs[i][0][zt]])
                m = [U[3 + j, zt, X, r0 : r0 + 8, :] for j in range(3)]
                s, mag = strain_of(d, m)
                for p, (a, b) in enumerate(PAIRS):
                    T[p, zt, 8 * t : 8 * t + 8, :] = u[a][zt] * u[b][zt]
                    T[6 + p, zt, 8 * t : 8 * t + 8, :] = (0.5 if a == b else 0.25) * mag * s[p]
                MB[X, zt, 8 * t : 8 * t + 8, :] = mag
        for p in range(12):
            for zt in range(2):
                for t in range(2):
                    r = 8 * t
                    YF[p, zt, X, r : r + 8, :] = (
                        T[p, zt, r : r + 8, :] + 2.0 * T[p, zt, r + 1 : r + 9, :] + T[p, zt, r + 2 : r + 10, :])
        return 0

    lax.fori_loop(1, nx + 3, stage_a, 0)

    def stage_y(X, _):
        for i in range(3):
            for zt in range(2):
                for t in range(3):
                    r = BASE - 1 + 8 * t
                    YV[i, zt, X, 8 * t : 8 * t + 8, :] = (
                        U[i, zt, X, r - 1 : r + 7, :] + 2.0 * U[i, zt, X, r : r + 8, :] + U[i, zt, X, r + 1 : r + 9, :])
        return 0

    lax.fori_loop(0, nx + 4, stage_y, 0)

    def stage_v(X, _):
        turn = 127 - 6 * X
        x_in = jnp.logical_and(jnp.logical_or(X >= 2, gx > 0), jnp.logical_or(X < nx + 2, gx < ngx - 1))
        for t in range(3):
            rr_ = row + 8 * t
            y_in = jnp.logical_and(rr_ >= jnp.where(gy > 0, 0, 1), rr_ < jnp.where(gy < ngy - 1, ny + 2, ny + 1))
            inside = jnp.logical_and(y_in, x_in)
            for i in range(3):
                a = [YV[i, zt, X - 1, 8 * t : 8 * t + 8, :] + 2.0 * YV[i, zt, X, 8 * t : 8 * t + 8, :]
                     + YV[i, zt, X + 1, 8 * t : 8 * t + 8, :] for zt in range(2)]
                prev, nxt = zshift(a, pltpu.roll(VE[i, 8 * t : 8 * t + 8, :], turn, 1))
                for zt in range(2):
                    v = (1.0 / 64.0) * (prev[zt] + 2.0 * a[zt] + nxt[zt])
                    VH[i, zt, X, 8 * t : 8 * t + 8, :] = jnp.where(inside, v, 0.0)
        return 0

    lax.fori_loop(1, nx + 3, stage_v, 0)

    LN[gz] = z8

    def stage_c(X, _):
        turn = 127 - 6 * X
        for t in range(2):
            r = 8 * t
            v = [[VH[i, zt, X, r + 1 : r + 9, :] for zt in range(2)] for i in range(3)]
            zs = [zshift(v[i], pltpu.roll(VHE[i, r + 1 : r + 9, :], turn, 1)) for i in range(3)]
            fl = []
            for p in range(12):
                a = [YF[p, zt, X - 1, r : r + 8, :] + 2.0 * YF[p, zt, X, r : r + 8, :]
                     + YF[p, zt, X + 1, r : r + 8, :] for zt in range(2)]
                prev, nxt = zshift(a, pltpu.roll(ZE[p, r : r + 8, :], turn, 1))
                fl.append([(1.0 / 64.0) * (prev[zt] + 2.0 * a[zt] + nxt[zt]) for zt in range(2)])
            num = den = None
            for zt in range(2):
                d = []
                for i in range(3):
                    ddx = VH[i, zt, X + 1, r + 1 : r + 9, :] - VH[i, zt, X - 1, r + 1 : r + 9, :]
                    ddy = VH[i, zt, X, r + 2 : r + 10, :] - VH[i, zt, X, r : r + 8, :]
                    d.append([ddx, ddy, zs[i][1][zt] - zs[i][0][zt]])
                m = [U[3 + j, zt, X, BASE + r : BASE + r + 8, :] for j in range(3)]
                s, mag = strain_of(d, m)
                delta = jnp.exp2((-2.0 / 3.0) * jnp.log2(m[0] * m[1] * m[2]))
                nn = dd = None
                for p, (a, b) in enumerate(PAIRS):
                    w = 1.0 if a == b else 2.0
                    leo = fl[p][zt] - v[a][zt] * v[b][zt]
                    q = fl[6 + p][zt] - (2.0 if a == b else 1.0) * mag * s[p]
                    wq = q if a == b else w * q
                    n_, d_ = wq * leo, wq * q
                    nn = n_ if nn is None else nn + n_
                    dd = d_ if dd is None else dd + d_
                d2 = 2.0 * delta
                n_, d_ = d2 * nn, d2 * d2 * dd
                num = n_ if num is None else num + n_
                den = d_ if den is None else den + d_
                DM[X - 2, zt, r : r + 8, :] = delta * MB[X, zt, r + 1 : r + 9, :]
            at = X - 2 + nx * t
            ln = jnp.where(lane == at, jnp.sum(num, axis=1, keepdims=True), LN[gz])
            LN[gz] = jnp.where(lane == at + 2 * nx, jnp.sum(den, axis=1, keepdims=True), ln)
        return 0

    lax.fori_loop(2, nx + 2, stage_c, 0)

    cps = []
    for k in range(1, ngz):
        cp = pltpu.make_async_remote_copy(
            src_ref=LN.at[gz], dst_ref=LN.at[gz], send_sem=ssem.at[20 + k], recv_sem=rsem.at[20 + gz],
            device_id={"gz": lax.rem(gz + k, ngz)}, device_id_type=MESH)
        cp.start()
        cps.append(cp)
    for k in range(1, ngz):
        src = lax.rem(gz + k, ngz)
        pltpu.make_async_remote_copy(
            src_ref=LN.at[gz], dst_ref=LN.at[src], send_sem=ssem.at[20 + k], recv_sem=rsem.at[20 + src],
            device_id={"gz": src}, device_id_type=MESH).wait_recv()
    tot = LN[0]
    for k in range(1, ngz):
        tot = tot + LN[k]
    tot = tot * (1.0 / (nz * ngz))
    den = pltpu.roll(tot, 128 - 2 * nx, 1)
    line = tot / (den + 1e-06)
    valid = lane < 2 * nx
    peak = jnp.max(jnp.where(valid, line, -jnp.inf), axis=0, keepdims=True)
    peak = jnp.max(peak, axis=1, keepdims=True)

    RX[me_c] = jnp.broadcast_to(peak, (1, 128))
    for k in range(1, nxc):
        c, dev = xc_dev(k)
        cp = pltpu.make_async_remote_copy(
            src_ref=RX.at[me_c], dst_ref=RX.at[me_c], send_sem=ssem.at[24 + k], recv_sem=rsem.at[24 + me_c],
            device_id=dev, device_id_type=MESH)
        cp.start()
        cps.append(cp)
    for k in range(1, nxc):
        c, dev = xc_dev(k)
        pltpu.make_async_remote_copy(
            src_ref=RX.at[me_c], dst_ref=RX.at[c], send_sem=ssem.at[24 + k], recv_sem=rsem.at[24 + c],
            device_id=dev, device_id_type=MESH).wait_recv()
    peak = RX[0]
    for k in range(1, nxc):
        peak = jnp.maximum(peak, RX[k])
    RZ[xz] = peak
    for k in range(1, nzc):
        c, dev = z_dev(k)
        cp = pltpu.make_async_remote_copy(
            src_ref=RZ.at[xz], dst_ref=RZ.at[xz], send_sem=ssem.at[32 + k], recv_sem=rsem.at[32 + xz],
            device_id=dev, device_id_type=MESH)
        cp.start()
        cps.append(cp)
    for k in range(1, nzc):
        c, dev = z_dev(k)
        pltpu.make_async_remote_copy(
            src_ref=RZ.at[xz], dst_ref=RZ.at[c], send_sem=ssem.at[32 + k], recv_sem=rsem.at[32 + c],
            device_id=dev, device_id_type=MESH).wait_recv()
    peak = RZ[0]
    for k in range(1, nzc):
        peak = jnp.maximum(peak, RZ[k])

    coef = jnp.minimum(line, 0.5 * peak)
    for x in range(nx):
        for t in range(2):
            at = x + nx * t
            cb = jnp.broadcast_to(coef[:, at : at + 1], (8, 128))
            for zt in range(2):
                visc[x, 8 * t : 8 * t + 8, 128 * zt : 128 * zt + 128] = cb * DM[x, zt, 8 * t : 8 * t + 8, :]
    ct = coef.T
    for t in range(2):
        coef_out[:, 8 * t : 8 * t + 8] = ct[nx * t : nx * t + nx, :]

    for cp in cps:
        cp.wait_send()
    for cp, cond in waits_send:
        if cond is None:
            cp.wait_send()
        else:
            pl.when(cond)(cp.wait_send)


def solution(mesh):
    sizes = tuple(mesh.shape[a] for a in ("gx", "gy", "gz"))
    ngx, ngy, ngz = sizes

    def per_device(velocity, metric):
        _, nx, ny, nz = velocity.shape
        vm = lambda *s: pltpu.VMEM(s, F32)
        return pl.pallas_call(
            functools.partial(kernel, sizes),
            out_shape=(jax.ShapeDtypeStruct((nx, ny, nz), F32), jax.ShapeDtypeStruct((nx, ny), F32)),
            in_specs=[pl.BlockSpec(memory_space=pl.ANY)] * 2,
            out_specs=(pl.BlockSpec(memory_space=pltpu.VMEM),) * 2,
            scratch_shapes=[
                vm(6, 2, nx + 4, PITCH, 128),
                vm(6, 16, 128),
                vm(2, 9, 2, nx, 128),
                vm(2, 9, 2, nx, 128),
                vm(4, 2, 16, 128),
                vm(4, 2, 16, 128),
                vm(2, 6, 16, 128),
                vm(6, 32, 128),
                vm(2, 16, 128),
                vm(2, 16, 128),
                vm(2, 16, 128),
                vm(2, 16, 128),
                vm(4, 8, 128),
                vm(12, 24, 128),
                vm(3, 24, 128),
                vm(12, 16, 128),
                vm(3, 24, 128),
                vm(3, 24, 128),
                vm(12, 2, 24, 128),
                vm(12, 2, nx + 4, 16, 128),
                vm(3, 2, nx + 4, 24, 128),
                vm(3, 2, nx + 4, 24, 128),
                vm(nx + 4, 2, 24, 128),
                vm(nx, 2, 16, 128),
                vm(ngz, 8, 128),
                vm(2 * ngy, 1, 128),
                vm(ngx // 2, 1, 128),
                vm(1, 128),
                pltpu.SemaphoreType.DMA((4,)),
                pltpu.SemaphoreType.DMA((40,)),
                pltpu.SemaphoreType.DMA((40,)),
            ],
            compiler_params=pltpu.CompilerParams(collective_id=0, has_side_effects=True),
        )(velocity, metric)

    return jax.shard_map(
        per_device,
        mesh=mesh,
        in_specs=(P(None, "gx", "gy", "gz"), P(None, "gx", "gy", "gz")),
        out_specs=(P("gx", "gy", "gz"), P("gx", "gy")),
        check_vma=False,
    )
```

time: 152 us -> 49.6 us (0.33)
  Pallas kernels: 0 us -> 46.5 us
  starting transfers between devices: 42 us -> 0 us
  waiting for transfers between devices: 38.7 us -> 0 us
  blocking collectives: 31 us -> 0 us
  other arithmetic: 19.5 us -> 0 us
  local copies, waits for them, and re-layouts: 17.9 us -> 2.28 us
    pallas_call x0 -> x1, Pallas kernels: none -> 46.5 us  [per_device(): pl.pallas_call(functools.partial(kernel, sizes), out_shape=(jax.ShapeDtyp...]
    ppermute x18 -> x0, starting transfers between devices: 42 us -> none  [the longest x4 15.1 us: with_halo_2(): lax.ppermute(last, axis, up)]
    ppermute x18 -> x0, waiting for transfers between devices: 38.7 us -> none  [the longest x5 20.3 us: with_halo(): lax.ppermute(lax.slice_in_dim(block, 0, width, axis=dim), axis, backward)]
    all_to_all x2 -> x0, blocking collectives: 31 us -> none  [from_everyone(): return lax.all_to_all(copies, axis, split_axis=0, concat_axis=0, tiled=True)]
    add x3 -> x0, other arithmetic: 9.52 us -> none  [box_three(): return 0.25 * lower_side + 0.5 * middle + 0.25 * upper_side]
    slice x11 -> x0, local copies, waits for them, and re-layouts: 5.71 us -> none  [the longest x4 2.17 us: with_halo_2(): leading = lax.slice_in_dim(x, 0, width, axis=dim)]
    unnamed x20 -> x4, local copies, waits for them, and re-layouts: 6.94 us -> 2.28 us
    ppermute x4 -> x0, local copies, waits for them, and re-layouts: 4.34 us -> none  [the longest x1 2.77 us: with_halo(): lax.ppermute(lax.slice_in_dim(block, 0, width, axis=dim), axis, backward)]
  transfers between devices with their start and end apart: 18 -> 0, of which waited for: 8 -> 0; matrix products, arithmetic and copies ran while one was open for 4% -> 0% of each run, Pallas kernels for 0% -> 0%
where the time goes in v1:
time: 49.6 us; the launch traced here: 49.5 us
  Pallas kernels  46.5 us (94%)
  local copies, waits for them, and re-layouts  2.28 us (5%)
  between operations  0.65 us (1%)
    pallas_call x1, Pallas kernels, per_device(): pl.pallas_call(functools.partial(kernel, sizes), out_shape=(jax.ShapeDtyp...  46.5 us
    unnamed x4, local copies, waits for them, and re-layouts  2.28 us

profile of v1, /device:TPU:1, one launch (start us, length us, event | category | flops | bytes accessed | tf_op | source)
XLA Modules:
  0.0 49.5 jit_solution(5387663461194418165)
XLA Ops:
  0.6 46.5 %shard_map.41 = (f32[16,16,256]{2,1,0:T(8,128)}, f32[16,16]{1,0:T(8,128)}) custom-call(f32[3,16,16,256]{3,2,1,0:T(8,128)} %vel.1, f32[3,16,16,256]{3,2,1,0:T(8,128)} %met.1), custom_call_target="tpu_custom_call" | custom-call | tf_op jit(solution)/shard_map/pallas_call | solution.py:499
  47.2 0.0 copy-start
  47.2 1.7 %copy.6 = f32[16,16,256]{2,1,0:T(8,128)} copy(f32[16,16,256]{2,1,0:T(8,128)} %get-tuple-element.4) | data formatting | bytes 524288
  48.9 0.0 copy-done
  48.9 0.6 %copy.7 = f32[16,16]{1,0:T(8,128)} copy(f32[16,16]{1,0:T(8,128)S(1)} %copy-done) | data formatting | bytes 2048
Async XLA Ops:
  47.2 1.7 %copy-start = (f32[16,16]{1,0:T(8,128)S(1)}, f32[16,16]{1,0:T(8,128)}, u32[]{:S(2)}) copy-start(f32[16,16]{1,0:T(8,128)} %get-tuple-element.5) | copy-start | bytes 3076

commit v2 on v1

--- a/solution.py
+++ b/solution.py
@@ -21,8 +21,8 @@
     return s, jnp.sqrt(0.5 * diag + 0.25 * off)
 
 
-def kernel(sizes, vel, met, visc, coef_out, U, O6, SY, RY, SC, RC, RO, ZG, SZX, RZX, SZY, RZY,
-           RZC, TZ, UE, ZE, VE, VHE, T, YF, YV, VH, MB, DM, LN, RX, RZ, PK, lsem, ssem, rsem):
+def kernel(sizes, vel, met, dm_out, line_out, half_out, U, O6, SY, RY, SC, RC, RO, ZG, SZX, RZX, SZY, RZY,
+           RZC, SZG, TZ, UE, ZE, VE, VHE, T, YF, YV, VH, MB, DM, LN, RX, RZ, lsem, ssem, rsem):
     ngx, ngy, ngz = sizes
     nx = vel.shape[1]
     ny = vel.shape[2]
@@ -43,18 +43,6 @@
             cp.start()
             ins.append(cp)
 
-    z8 = jnp.zeros((8, 128), F32)
-    for f in range(6):
-        for zt in range(2):
-            for X in (0, 1, nx + 2, nx + 3):
-                for r in range(0, ny, 8):
-                    U[f, zt, X, BASE + r : BASE + r + 8, :] = z8
-    RY[...] = jnp.zeros(RY.shape, F32)
-    RC[...] = jnp.zeros(RC.shape, F32)
-    RZX[...] = jnp.zeros(RZX.shape, F32)
-    RZY[...] = jnp.zeros(RZY.shape, F32)
-    RZC[...] = jnp.zeros(RZC.shape, F32)
-
     bar = pltpu.get_barrier_semaphore()
 
     def greet(dev):
@@ -66,21 +54,31 @@
     def dy(s):
         return gy + (1 if s else -1)
 
-    for k in range(1, ngz):
-        greet({"gz": lax.rem(gz + k, ngz)})
-    for s in range(2):
+    def gz_at(d):
+        return lax.rem(gz + d + ngz, ngz)
+
+    both = {(sx, sy): jnp.logical_and(has["x", sx], has["y", sy]) for sx in range(2) for sy in range(2)}
+    for d in (-1, 1):
+        greet({"gz": gz_at(d)})
+    for s in range(2):
+        @pl.when(has["y", s])
+        def _():
+            for d in (-1, 0, 1):
+                greet({"gy": dy(s), "gz": gz_at(d)})
+
         @pl.when(has["x", s])
         def _():
-            greet({"gx": dx(s)})
-
-        @pl.when(has["y", s])
-        def _():
-            greet({"gy": dy(s)})
+            for d in (-1, 0, 1):
+                greet({"gx": dx(s), "gz": gz_at(d)})
 
         for q in range(2):
-            @pl.when(jnp.logical_and(has["x", s], has["y", q]))
+            @pl.when(both[s, q])
             def _():
-                greet({"gx": dx(s), "gy": dy(q)})
+                for d in (-1, 0, 1):
+                    greet({"gx": dx(s), "gy": dy(q), "gz": gz_at(d)})
+
+    for k in range(2, ngz - 1):
+        greet({"gz": gz_at(k)})
 
     nxc = 2 * ngy
     me_c = xlo * ngy + gy
@@ -99,6 +97,32 @@
         greet(z_dev(k)[1])
     ex = has["x", 0].astype(jnp.int32) + has["x", 1].astype(jnp.int32)
     ey = has["y", 0].astype(jnp.int32) + has["y", 1].astype(jnp.int32)
+    partners = 3 * (1 + ex) * (1 + ey) - 1 + max(ngz - 3, 0) + (nxc - 1) + (nzc - 1)
+
+    z8 = jnp.zeros((8, 128), F32)
+    for s in range(2):
+        @pl.when(jnp.logical_not(has["x", s]))
+        def _():
+            for f in range(6):
+                for zt in range(2):
+                    for X in ((nx + 2, nx + 3) if s else (0, 1)):
+                        for r in range(0, ny, 8):
+                            U[f, zt, X, BASE + r : BASE + r + 8, :] = z8
+            for d in range(3):
+                RZX[d, s] = jnp.zeros(RZX.shape[2:], F32)
+
+        @pl.when(jnp.logical_not(has["y", s]))
+        def _():
+            RY[s] = jnp.zeros(RY.shape[1:], F32)
+            for d in range(3):
+                RZY[d, s] = jnp.zeros(RZY.shape[2:], F32)
+
+        for q in range(2):
+            @pl.when(jnp.logical_not(both[s, q]))
+            def _():
+                RC[2 * s + q] = jnp.zeros(RC.shape[1:], F32)
+                for d in range(3):
+                    RZC[d, 2 * s + q] = z8
 
     lane = lax.broadcasted_iota(jnp.int32, (8, 128), 1)
     lx = lax.shift_right_logical(lane * 43, 8)
@@ -117,6 +141,19 @@
             O6[f, 8 * t : 8 * t + 8, :] = acc
 
     for s in range(2):
+        first = 6 * (nx if s else 2)
+        for t in range(2):
+            acc = z8
+            for f in range(6):
+                part = pltpu.roll(O6[f, 8 * t : 8 * t + 8, :], (12 * f - first) % 128, 1)
+                acc = jnp.where(jnp.logical_and(lane >= 12 * f, lane < 12 * f + 12), part, acc)
+            SZX[s, 8 * t : 8 * t + 8, :] = acc
+        y = ny - 2 if s else 0
+        for f in range(6):
+            SZY[s, 2 * f : 2 * f + 2, :] = O6[f, y : y + 2, :]
+        SZY[s, 12:16, :] = z8[0:4]
+
+    for s in range(2):
         for f in range(6):
             for k in range(2):
                 if f >= 3 and k != s:
@@ -148,7 +185,7 @@
                 for zt in range(2):
                     SC[2 * sx + sy, zt, r : r + 1, :] = U[f, zt, X, yr : yr + 1, :]
 
-    pl.semaphore_wait(bar, (ngz - 1) + (nxc - 1) + (nzc - 1) + ex + ey + ex * ey)
+    pl.semaphore_wait(bar, partners)
 
     waits_send, waits_recv = [], {}
 
@@ -171,15 +208,22 @@
             pl.when(cond)(cp.wait_recv)
 
     for s in range(2):
-        put(s, O6, RO.at[1 - s], {"gz": lax.rem(gz + (1 if s else ngz - 1), ngz)})
+        put(s, O6, RO.at[1 - s], {"gz": gz_at(1 if s else -1)})
+    for i, d in enumerate((-1, 0, 1)):
+        o = 2 - i
+        for s in range(2):
+            put(12 + 2 * i + s, SZY.at[s], RZY.at[o, 1 - s], {"gy": dy(s), "gz": gz_at(d)},
+                has["y", s], has["y", 1 - s])
+            put(18 + 2 * i + s, SZX.at[s], RZX.at[o, 1 - s], {"gx": dx(s), "gz": gz_at(d)},
+                has["x", s], has["x", 1 - s])
+        for sx in range(2):
+            for sy in range(2):
+                put(24 + 4 * i + 2 * sx + sy, SZX.at[sx, pl.ds(ny - 8 if sy else 0, 8), :],
+                    RZC.at[o, 2 * (1 - sx) + 1 - sy],
+                    {"gx": dx(sx), "gy": dy(sy), "gz": gz_at(d)},
+                    both[sx, sy], both[1 - sx, 1 - sy])
     for s in range(2):
         put(2 + s, SY.at[s], RY.at[1 - s], {"gy": dy(s)}, has["y", s], has["y", 1 - s])
-    for sx in range(2):
-        for sy in range(2):
-            c, o = 2 * sx + sy, 2 * (1 - sx) + 1 - sy
-            put(8 + c, SC.at[c], RC.at[o], {"gx": dx(sx), "gy": dy(sy)},
-                jnp.logical_and(has["x", sx], has["y", sy]),
-                jnp.logical_and(has["x", 1 - sx], has["y", 1 - sy]))
     rr = pl.ds(BASE, ny)
     for s in range(2):
         far, near = (nx, nx + 1) if s else (3, 2)
@@ -188,85 +232,41 @@
             has["x", s], has["x", 1 - s])
         put(6 + s, U.at[pl.ds(0, 3), :, far, rr, :], U.at[pl.ds(0, 3), :, gfar, rr, :],
             {"gx": dx(s)}, has["x", s], has["x", 1 - s])
-
-    got(0)
-    got(1)
-    lanes_x = jnp.logical_and(lx >= 2, lx < nx + 2)
+    for sx in range(2):
+        for sy in range(2):
+            put(8 + 2 * sx + sy, SC.at[2 * sx + sy], RC.at[2 * (1 - sx) + 1 - sy],
+                {"gx": dx(sx), "gy": dy(sy)}, both[sx, sy], both[1 - sx, 1 - sy])
+
+    def comb(left, own, right):
+        return jnp.where(lc < 2, left, jnp.where(lc == 2, own, pltpu.roll(jnp.where(lc == 1, own, right), 2, 1)))
+
+    for n in (0, 1, *range(12, 36)):
+        got(n)
+    zx, zc = {}, {}
+    for s in range(2):
+        for t in range(2):
+            rows = slice(8 * t, 8 * t + 8)
+            zx[s, t] = comb(RZX[0, s, rows, :], RZX[1, s, rows, :], RZX[2, s, rows, :])
+            SZG[s, rows, :] = comb(RZY[0, s, rows, :], RZY[1, s, rows, :], RZY[2, s, rows, :])
+    for c in range(4):
+        zc[c] = comb(RZC[0, c], RZC[1, c], RZC[2, c])
     for f in range(6):
         ZG[f, 0:8, :] = z8
         ZG[f, 24:32, :] = z8
         for t in range(2):
             rows = slice(8 * t, 8 * t + 8)
-            own = O6[f, rows, :]
-            right = pltpu.roll(jnp.where(lc == 1, own, RO[1, f, rows, :]), 2, 1)
-            z = jnp.where(lc < 2, RO[0, f, rows, :], jnp.where(lc == 2, own, right))
-            ZG[f, BASE + 8 * t : BASE + 8 * t + 8, :] = jnp.where(lanes_x, z, 0.0)
-    for s in range(2):
-        first = 6 * (nx if s else 2)
-        for t in range(2):
-            acc = z8
-            for f in range(6):
-                part = pltpu.roll(ZG[f, BASE + 8 * t : BASE + 8 * t + 8, :], (12 * f - first) % 128, 1)
-                acc = jnp.where(jnp.logical_and(lane >= 12 * f, lane < 12 * f + 12), part, acc)
-            SZX[s, 8 * t : 8 * t + 8, :] = acc
-        y = ny - 2 if s else 0
-        for f in range(6):
-            SZY[s, 2 * f : 2 * f + 2, :] = ZG[f, BASE + y : BASE + y + 2, :]
-    for s in range(2):
-        put(14 + s, SZY.at[s], RZY.at[1 - s], {"gy": dy(s)}, has["y", s], has["y", 1 - s])
-        put(12 + s, SZX.at[s], RZX.at[1 - s], {"gx": dx(s)}, has["x", s], has["x", 1 - s])
-    for sx in range(2):
-        for sy in range(2):
-            c, o = 2 * sx + sy, 2 * (1 - sx) + 1 - sy
-            put(16 + c, SZX.at[sx, pl.ds(ny - 8 if sy else 0, 8), :], RZC.at[o],
-                {"gx": dx(sx), "gy": dy(sy)},
-                jnp.logical_and(has["x", sx], has["y", sy]),
-                jnp.logical_and(has["x", 1 - sx], has["y", 1 - sy]))
-
-    for n in range(2, 20):
-        got(n)
-
-    for s in range(2):
-        for f in range(6):
-            for k in range(2):
-                if f >= 3 and k == s:
-                    continue
-                y = (ny + k) if s else k - 2
-                slab = 2 * f + k if f < 3 else 3 + f
-                for zt in range(2):
-                    U[f, zt, pl.ds(2, nx), BASE + y, :] = RY[s, slab, zt, :, :]
-    for sx in range(2):
-        for sy in range(2):
-            src = {}
-            r = 0
-            for f in range(6):
-                for kx in range(2):
-                    for ky in range(2):
-                        if f >= 3 and (kx != 1 - sx or ky != 1 - sy):
-                            continue
-                        src[f, kx, ky] = r
-                        r += 1
-            for (f, kx, ky), r in src.items():
-                X = (nx + 2 if sx else 0) + kx
-                yr = (ny if sy else -2) + ky + BASE
-                for zt in range(2):
-                    U[f, zt, X, yr : yr + 1, :] = RC[2 * sx + sy, zt, r : r + 1, :]
-    for f in range(6):
-        for t in range(2):
-            rows = slice(BASE + 8 * t, BASE + 8 * t + 8)
-            z = ZG[f, rows, :]
+            z = comb(RO[0, f, rows, :], O6[f, rows, :], RO[1, f, rows, :])
             for s in range(2):
                 at = 6 * (nx + 2) if s else 0
-                part = pltpu.roll(RZX[s, 8 * t : 8 * t + 8, :], (at - 12 * f) % 128, 1)
+                part = pltpu.roll(zx[s, t], (at - 12 * f) % 128, 1)
                 z = jnp.where(jnp.logical_and(lane >= at, lane < at + 12), part, z)
-            ZG[f, rows, :] = z
+            ZG[f, BASE + 8 * t : BASE + 8 * t + 8, :] = z
         for sy in range(2):
             yr = BASE + (ny if sy else -2)
-            z = RZY[sy, 2 * f : 2 * f + 2, :]
+            z = SZG[sy, 2 * f : 2 * f + 2, :]
             for sx in range(2):
                 at = 6 * (nx + 2) if sx else 0
-                tile = RZC[2 * sx + sy]
-                part = pltpu.roll(tile, (at - 12 * f) % 128, 1)
+                part = pltpu.roll(zc[2 * sx + sy], (at - 12 * f) % 128, 1)
                 part = part[0:2] if sy else part[6:8]
                 lane2 = lane[0:2]
                 z = jnp.where(jnp.logical_and(lane2 >= at, lane2 < at + 12), part, z)
@@ -338,7 +338,6 @@
                         T[p, zt, r : r + 8, :] + 2.0 * T[p, zt, r + 1 : r + 9, :] + T[p, zt, r + 2 : r + 10, :])
         return 0
 
-    lax.fori_loop(1, nx + 3, stage_a, 0)
 
     def stage_y(X, _):
         for i in range(3):
@@ -349,7 +348,6 @@
                         U[i, zt, X, r - 1 : r + 7, :] + 2.0 * U[i, zt, X, r : r + 8, :] + U[i, zt, X, r + 1 : r + 9, :])
         return 0
 
-    lax.fori_loop(0, nx + 4, stage_y, 0)
 
     def stage_v(X, _):
         turn = 127 - 6 * X
@@ -367,9 +365,6 @@
                     VH[i, zt, X, 8 * t : 8 * t + 8, :] = jnp.where(inside, v, 0.0)
         return 0
 
-    lax.fori_loop(1, nx + 3, stage_v, 0)
-
-    LN[gz] = z8
 
     def stage_c(X, _):
         turn = 127 - 6 * X
@@ -412,19 +407,67 @@
             LN[gz] = jnp.where(lane == at + 2 * nx, jnp.sum(den, axis=1, keepdims=True), ln)
         return 0
 
-    lax.fori_loop(2, nx + 2, stage_c, 0)
+    LN[gz] = z8
+    got(2)
+    got(3)
+    for s in range(2):
+        for f in range(6):
+            for k in range(2):
+                if f >= 3 and k == s:
+                    continue
+                y = (ny + k) if s else k - 2
+                slab = 2 * f + k if f < 3 else 3 + f
+                for zt in range(2):
+                    U[f, zt, pl.ds(2, nx), BASE + y, :] = RY[s, slab, zt, :, :]
+    lax.fori_loop(3, nx + 1, stage_a, 0)
+    lax.fori_loop(2, nx + 2, stage_y, 0)
+    lax.fori_loop(3, nx + 1, stage_v, 0)
+    lax.fori_loop(4, nx, stage_c, 0)
+
+    for n in range(4, 12):
+        got(n)
+    for sx in range(2):
+        for sy in range(2):
+            src = {}
+            r = 0
+            for f in range(6):
+                for kx in range(2):
+                    for ky in range(2):
+                        if f >= 3 and (kx != 1 - sx or ky != 1 - sy):
+                            continue
+                        src[f, kx, ky] = r
+                        r += 1
+            for (f, kx, ky), r in src.items():
+                X = (nx + 2 if sx else 0) + kx
+                yr = (ny if sy else -2) + ky + BASE
+                for zt in range(2):
+                    U[f, zt, X, yr : yr + 1, :] = RC[2 * sx + sy, zt, r : r + 1, :]
+
+    def ends(a, stage):
+        lax.fori_loop(0, 4, lambda k, c: stage(jnp.where(k < 2, a + k, nx - a + k), c), 0)
+
+    ends(1, stage_a)
+    ends(0, stage_y)
+    ends(1, stage_v)
+    ends(2, stage_c)
+
+    outs = []
+    for zt in range(2):
+        cp = pltpu.make_async_copy(DM.at[:, zt], dm_out.at[:, :, pl.ds(128 * zt, 128)], lsem.at[4 + zt])
+        cp.start()
+        outs.append(cp)
 
     cps = []
     for k in range(1, ngz):
         cp = pltpu.make_async_remote_copy(
-            src_ref=LN.at[gz], dst_ref=LN.at[gz], send_sem=ssem.at[20 + k], recv_sem=rsem.at[20 + gz],
+            src_ref=LN.at[gz], dst_ref=LN.at[gz], send_sem=ssem.at[40 + k], recv_sem=rsem.at[40 + gz],
             device_id={"gz": lax.rem(gz + k, ngz)}, device_id_type=MESH)
         cp.start()
         cps.append(cp)
     for k in range(1, ngz):
         src = lax.rem(gz + k, ngz)
         pltpu.make_async_remote_copy(
-            src_ref=LN.at[gz], dst_ref=LN.at[src], send_sem=ssem.at[20 + k], recv_sem=rsem.at[20 + src],
+            src_ref=LN.at[gz], dst_ref=LN.at[src], send_sem=ssem.at[40 + k], recv_sem=rsem.at[40 + src],
             device_id={"gz": src}, device_id_type=MESH).wait_recv()
     tot = LN[0]
     for k in range(1, ngz):
@@ -440,14 +483,14 @@
     for k in range(1, nxc):
         c, dev = xc_dev(k)
         cp = pltpu.make_async_remote_copy(
-            src_ref=RX.at[me_c], dst_ref=RX.at[me_c], send_sem=ssem.at[24 + k], recv_sem=rsem.at[24 + me_c],
+            src_ref=RX.at[me_c], dst_ref=RX.at[me_c], send_sem=ssem.at[44 + k], recv_sem=rsem.at[44 + me_c],
             device_id=dev, device_id_type=MESH)
         cp.start()
         cps.append(cp)
     for k in range(1, nxc):
         c, dev = xc_dev(k)
         pltpu.make_async_remote_copy(
-            src_ref=RX.at[me_c], dst_ref=RX.at[c], send_sem=ssem.at[24 + k], recv_sem=rsem.at[24 + c],
+            src_ref=RX.at[me_c], dst_ref=RX.at[c], send_sem=ssem.at[44 + k], recv_sem=rsem.at[44 + c],
             device_id=dev, device_id_type=MESH).wait_recv()
     peak = RX[0]
     for k in range(1, nxc):
@@ -456,29 +499,25 @@
     for k in range(1, nzc):
         c, dev = z_dev(k)
         cp = pltpu.make_async_remote_copy(
-            src_ref=RZ.at[xz], dst_ref=RZ.at[xz], send_sem=ssem.at[32 + k], recv_sem=rsem.at[32 + xz],
+            src_ref=RZ.at[xz], dst_ref=RZ.at[xz], send_sem=ssem.at[52 + k], recv_sem=rsem.at[52 + xz],
             device_id=dev, device_id_type=MESH)
         cp.start()
         cps.append(cp)
     for k in range(1, nzc):
         c, dev = z_dev(k)
         pltpu.make_async_remote_copy(
-            src_ref=RZ.at[xz], dst_ref=RZ.at[c], send_sem=ssem.at[32 + k], recv_sem=rsem.at[32 + c],
+            src_ref=RZ.at[xz], dst_ref=RZ.at[c], send_sem=ssem.at[52 + k], recv_sem=rsem.at[52 + c],
             device_id=dev, device_id_type=MESH).wait_recv()
     peak = RZ[0]
     for k in range(1, nzc):
         peak = jnp.maximum(peak, RZ[k])
 
-    coef = jnp.minimum(line, 0.5 * peak)
-    for x in range(nx):
-        for t in range(2):
-            at = x + nx * t
-            cb = jnp.broadcast_to(coef[:, at : at + 1], (8, 128))
-            for zt in range(2):
-                visc[x, 8 * t : 8 * t + 8, 128 * zt : 128 * zt + 128] = cb * DM[x, zt, 8 * t : 8 * t + 8, :]
-    ct = coef.T
+    half_out[...] = 0.5 * peak
+    lt = line.T
     for t in range(2):
-        coef_out[:, 8 * t : 8 * t + 8] = ct[nx * t : nx * t + nx, :]
+        line_out[:, 8 * t : 8 * t + 8] = lt[nx * t : nx * t + nx, :]
+    for cp in outs:
+        cp.wait()
 
     for cp in cps:
         cp.wait_send()
@@ -496,11 +535,12 @@
     def per_device(velocity, metric):
         _, nx, ny, nz = velocity.shape
         vm = lambda *s: pltpu.VMEM(s, F32)
-        return pl.pallas_call(
+        dm, line, half = pl.pallas_call(
             functools.partial(kernel, sizes),
-            out_shape=(jax.ShapeDtypeStruct((nx, ny, nz), F32), jax.ShapeDtypeStruct((nx, ny), F32)),
+            out_shape=(jax.ShapeDtypeStruct((nx, ny, nz), F32), jax.ShapeDtypeStruct((nx, ny), F32),
+                       jax.ShapeDtypeStruct((1, 128), F32)),
             in_specs=[pl.BlockSpec(memory_space=pl.ANY)] * 2,
-            out_specs=(pl.BlockSpec(memory_space=pltpu.VMEM),) * 2,
+            out_specs=(pl.BlockSpec(memory_space=pl.ANY),) + (pl.BlockSpec(memory_space=pltpu.VMEM),) * 2,
             scratch_shapes=[
                 vm(6, 2, nx + 4, PITCH, 128),
                 vm(6, 16, 128),
@@ -511,10 +551,11 @@
                 vm(2, 6, 16, 128),
                 vm(6, 32, 128),
                 vm(2, 16, 128),
+                vm(3, 2, 16, 128),
                 vm(2, 16, 128),
+                vm(3, 2, 16, 128),
+                vm(3, 4, 8, 128),
                 vm(2, 16, 128),
-                vm(2, 16, 128),
-                vm(4, 8, 128),
                 vm(12, 24, 128),
                 vm(3, 24, 128),
                 vm(12, 16, 128),
@@ -529,13 +570,14 @@
                 vm(ngz, 8, 128),
                 vm(2 * ngy, 1, 128),
                 vm(ngx // 2, 1, 128),
-                vm(1, 128),
-                pltpu.SemaphoreType.DMA((4,)),
-                pltpu.SemaphoreType.DMA((40,)),
-                pltpu.SemaphoreType.DMA((40,)),
+                pltpu.SemaphoreType.DMA((6,)),
+                pltpu.SemaphoreType.DMA((60,)),
+                pltpu.SemaphoreType.DMA((60,)),
             ],
             compiler_params=pltpu.CompilerParams(collective_id=0, has_side_effects=True),
         )(velocity, metric)
+        coefficient = jnp.minimum(line, half[0, 0])
+        return coefficient[:, :, None] * dm, coefficient
 
     return jax.shard_map(
         per_device,

time: 49.6 us -> 49.8 us (level)
  other arithmetic: 0 us -> 1.79 us
  local copies, waits for them, and re-layouts: 2.28 us -> 0.69 us
    mul x0 -> x1, other arithmetic: none -> 1.75 us  [per_device(): return (coefficient[:, :, None] * dm, coefficient)]
    unnamed x4 -> x6, local copies, waits for them, and re-layouts: 2.28 us -> 0.69 us
where the time goes in v2:
time: 49.8 us; the launch traced here: 49.6 us
  Pallas kernels  46.5 us (93%)
  other arithmetic  1.79 us (4%)
  local copies, waits for them, and re-layouts  0.69 us (1%)
  between operations  0.67 us (1%)
    pallas_call x1, Pallas kernels, per_device(): pl.pallas_call(functools.partial(kernel, sizes), out_shape=(jax.ShapeDtyp...  46.5 us
    mul x1, other arithmetic, per_device(): return (coefficient[:, :, None] * dm, coefficient)  1.75 us

profile of v2, /device:TPU:1, one launch (start us, length us, event | category | flops | bytes accessed | tf_op | source)
XLA Modules:
  0.0 49.6 jit_solution(11314172932624912477)
XLA Ops:
  0.6 46.5 %shard_map.41 = (f32[16,16,256]{2,1,0:T(8,128)}, f32[16,16]{1,0:T(8,128)}, f32[1,128]{1,0:T(1,128)}) custom-call(f32[3,16,16,256]{3,2,1,0:T(8,128)} %vel.1, f32[3,16,16,256]{3,2,1,0:T(8,128)} %met.1), custom_call_target="tpu_custom_call" | custom-call | tf_op jit(solution)/shard_map/pallas_call | solution.py:538
  47.1 0.0 copy-start.1
  47.1 0.0 copy-start.2
  47.1 0.7 %copy-done.1 = f32[16,16]{1,0:T(8,128)S(1)} copy-done((f32[16,16]{1,0:T(8,128)S(1)}, f32[16,16]{1,0:T(8,128)}, u32[]{:S(2)}) %copy-start.1) | copy-done | bytes 1048
  47.8 0.0 copy-done.2
  47.9 0.0 copy-start
  47.9 1.8 %broadcast_multiply_fusion = f32[16,16,256]{2,1,0:T(8,128)} fusion(f32[16,16,256]{2,1,0:T(8,128)} %get-tuple-element.7, f32[16,16]{1,0:T(8,128)S(1)} %broadcast_minimum_fusion), kind=kLoop, calls=%fused_computation | loop fusion | flops 65536 | bytes 525312 | tf_op jit(solution)/shard_map/mul | solution.py:580
  49.6 0.0 copy-done
  (1 shorter events, 0.0 us)
Async XLA Ops:
  47.1 0.7 %copy-start.1 = (f32[16,16]{1,0:T(8,128)S(1)}, f32[16,16]{1,0:T(8,128)}, u32[]{:S(2)}) copy-start(f32[16,16]{1,0:T(8,128)} %get-tuple-element.5) | copy-start | bytes 3076
  47.1 0.7 %copy-start.2 = (f32[1,128]{1,0:T(1,128)S(1)}, f32[1,128]{1,0:T(1,128)}, u32[]{:S(2)}) copy-start(f32[1,128]{1,0:T(1,128)} %get-tuple-element.6) | copy-start | bytes 1540
  47.9 1.8 %copy-start = (f32[16,16]{1,0:T(8,128)}, f32[16,16]{1,0:T(8,128)S(1)}, u32[]{:S(2)}) copy-start(f32[16,16]{1,0:T(8,128)S(1)} %broadcast_minimum_fusion) | copy-start | bytes 3076

commit v3 on v2

--- a/solution.py
+++ b/solution.py
@@ -124,12 +124,47 @@
                 for d in range(3):
                     RZC[d, 2 * s + q] = z8
 
+    for cp in ins:
+        cp.wait()
+    for s in range(2):
+        for f in range(6):
+            for k in range(2):
+                if f >= 3 and k != s:
+                    continue
+                y = (ny - 2 + k) if s else k
+                slab = 2 * f + k if f < 3 else 3 + f
+                for zt in range(2):
+                    SY[s, slab, zt, :, :] = U[f, zt, pl.ds(2, nx), BASE + y, :]
+
+    pl.semaphore_wait(bar, partners)
+
+    waits_send, waits_recv = [], {}
+
+    def put(n, src, dst, dev, send_if=None, recv_if=None):
+        cp = pltpu.make_async_remote_copy(
+            src_ref=src, dst_ref=dst, send_sem=ssem.at[n], recv_sem=rsem.at[n],
+            device_id=dev, device_id_type=MESH)
+        if send_if is None:
+            cp.start()
+        else:
+            pl.when(send_if)(cp.start)
+        waits_send.append((cp, send_if))
+        waits_recv[n] = (cp, recv_if)
+
+    def got(n):
+        cp, cond = waits_recv[n]
+        if cond is None:
+            cp.wait_recv()
+        else:
+            pl.when(cond)(cp.wait_recv)
+
+    for s in range(2):
+        put(2 + s, SY.at[s], RY.at[1 - s], {"gy": dy(s)}, has["y", s], has["y", 1 - s])
+
     lane = lax.broadcasted_iota(jnp.int32, (8, 128), 1)
     lx = lax.shift_right_logical(lane * 43, 8)
     lc = lane - 6 * lx
     row = lax.broadcasted_iota(jnp.int32, (8, 128), 0)
-    for cp in ins:
-        cp.wait()
     half = lane < 64
     for f in range(6):
         for t in range(2):
@@ -152,16 +187,6 @@
         for f in range(6):
             SZY[s, 2 * f : 2 * f + 2, :] = O6[f, y : y + 2, :]
         SZY[s, 12:16, :] = z8[0:4]
-
-    for s in range(2):
-        for f in range(6):
-            for k in range(2):
-                if f >= 3 and k != s:
-                    continue
-                y = (ny - 2 + k) if s else k
-                slab = 2 * f + k if f < 3 else 3 + f
-                for zt in range(2):
-                    SY[s, slab, zt, :, :] = U[f, zt, pl.ds(2, nx), BASE + y, :]
 
     def corner_rows(out, sx, sy):
         r = 0
@@ -185,27 +210,6 @@
                 for zt in range(2):
                     SC[2 * sx + sy, zt, r : r + 1, :] = U[f, zt, X, yr : yr + 1, :]
 
-    pl.semaphore_wait(bar, partners)
-
-    waits_send, waits_recv = [], {}
-
-    def put(n, src, dst, dev, send_if=None, recv_if=None):
-        cp = pltpu.make_async_remote_copy(
-            src_ref=src, dst_ref=dst, send_sem=ssem.at[n], recv_sem=rsem.at[n],
-            device_id=dev, device_id_type=MESH)
-        if send_if is None:
-            cp.start()
-        else:
-            pl.when(send_if)(cp.start)
-        waits_send.append((cp, send_if))
-        waits_recv[n] = (cp, recv_if)
-
-    def got(n):
-        cp, cond = waits_recv[n]
-        if cond is None:
-            cp.wait_recv()
-        else:
-            pl.when(cond)(cp.wait_recv)
 
     for s in range(2):
         put(s, O6, RO.at[1 - s], {"gz": gz_at(1 if s else -1)})
@@ -222,21 +226,6 @@
                     RZC.at[o, 2 * (1 - sx) + 1 - sy],
                     {"gx": dx(sx), "gy": dy(sy), "gz": gz_at(d)},
                     both[sx, sy], both[1 - sx, 1 - sy])
-    for s in range(2):
-        put(2 + s, SY.at[s], RY.at[1 - s], {"gy": dy(s)}, has["y", s], has["y", 1 - s])
-    rr = pl.ds(BASE, ny)
-    for s in range(2):
-        far, near = (nx, nx + 1) if s else (3, 2)
-        gfar, gnear = (0, 1) if s else (nx + 3, nx + 2)
-        put(4 + s, U.at[:, :, near, rr, :], U.at[:, :, gnear, rr, :], {"gx": dx(s)},
-            has["x", s], has["x", 1 - s])
-        put(6 + s, U.at[pl.ds(0, 3), :, far, rr, :], U.at[pl.ds(0, 3), :, gfar, rr, :],
-            {"gx": dx(s)}, has["x", s], has["x", 1 - s])
-    for sx in range(2):
-        for sy in range(2):
-            put(8 + 2 * sx + sy, SC.at[2 * sx + sy], RC.at[2 * (1 - sx) + 1 - sy],
-                {"gx": dx(sx), "gy": dy(sy)}, both[sx, sy], both[1 - sx, 1 - sy])
-
     def comb(left, own, right):
         return jnp.where(lc < 2, left, jnp.where(lc == 2, own, pltpu.roll(jnp.where(lc == 1, own, right), 2, 1)))
 
@@ -410,6 +399,19 @@
     LN[gz] = z8
     got(2)
     got(3)
+    rr = pl.ds(BASE, ny)
+    for s in range(2):
+        far, near = (nx, nx + 1) if s else (3, 2)
+        gfar, gnear = (0, 1) if s else (nx + 3, nx + 2)
+        put(4 + s, U.at[:, :, near, rr, :], U.at[:, :, gnear, rr, :], {"gx": dx(s)},
+            has["x", s], has["x", 1 - s])
+        put(6 + s, U.at[pl.ds(0, 3), :, far, rr, :], U.at[pl.ds(0, 3), :, gfar, rr, :],
+            {"gx": dx(s)}, has["x", s], has["x", 1 - s])
+    for sx in range(2):
+        for sy in range(2):
+            put(8 + 2 * sx + sy, SC.at[2 * sx + sy], RC.at[2 * (1 - sx) + 1 - sy],
+                {"gx": dx(sx), "gy": dy(sy)}, both[sx, sy], both[1 - sx, 1 - sy])
+
     for s in range(2):
         for f in range(6):
             for k in range(2):
@@ -537,8 +539,7 @@
         vm = lambda *s: pltpu.VMEM(s, F32)
         dm, line, half = pl.pallas_call(
             functools.partial(kernel, sizes),
-            out_shape=(jax.ShapeDtypeStruct((nx, ny, nz), F32), jax.ShapeDtypeStruct((nx, ny), F32),
-                       jax.ShapeDtypeStruct((1, 128), F32)),
+            out_shape=(vm(nx, ny, nz), vm(nx, ny), vm(1, 128)),
             in_specs=[pl.BlockSpec(memory_space=pl.ANY)] * 2,
             out_specs=(pl.BlockSpec(memory_space=pl.ANY),) + (pl.BlockSpec(memory_space=pltpu.VMEM),) * 2,
             scratch_shapes=[

time: 49.8 us -> 43.2 us (0.87)
  Pallas kernels: 46.5 us -> 41.6 us
  other arithmetic: 1.79 us -> 0.84 us
  local copies, waits for them, and re-layouts: 0.69 us -> 0.01 us
    pallas_call x1, Pallas kernels: 46.5 us -> 41.6 us  [per_device(): pl.pallas_call(functools.partial(kernel, sizes), out_shape=(vm(nx, ny, nz...]
    mul x1, other arithmetic: 1.75 us -> 0.81 us  [per_device(): return (coefficient[:, :, None] * dm, coefficient)]
    unnamed x6 -> x2, local copies, waits for them, and re-layouts: 0.69 us -> 0.01 us
where the time goes in v3:
time: 43.2 us; the launch traced here: 43.1 us
  Pallas kernels  41.6 us (96%)
  other arithmetic  0.84 us (2%)
  between operations  0.65 us (2%)
    pallas_call x1, Pallas kernels, per_device(): pl.pallas_call(functools.partial(kernel, sizes), out_shape=(vm(nx, ny, nz...  41.6 us

profile of v3, /device:TPU:1, one launch (start us, length us, event | category | flops | bytes accessed | tf_op | source)
XLA Modules:
  0.0 43.1 jit_solution(4780080163650305375)
XLA Ops:
  0.6 41.6 %shard_map.41 = (f32[16,16,256]{2,1,0:T(8,128)S(1)}, f32[16,16]{1,0:T(8,128)S(1)}, f32[1,128]{1,0:T(1,128)S(1)}) custom-call(f32[3,16,16,256]{3,2,1,0:T(8,128)} %vel.1, f32[3,16,16,256]{3,2,1,0:T(8,128)} %met.1), custom_call_target="tpu_custom_call" | custom-call | tf_op jit(solution)/shard_map/pallas_call | solution.py:540
  42.3 0.0 copy-start
  42.3 0.8 %broadcast_multiply_fusion = f32[16,16,256]{2,1,0:T(8,128)} fusion(f32[16,16,256]{2,1,0:T(8,128)S(1)} %get-tuple-element.7, f32[16,16]{1,0:T(8,128)S(1)} %broadcast_minimum_fusion), kind=kLoop, calls=%fused_computation | loop fusion | flops 65536 | bytes 525312 | tf_op jit(solution)/shard_map/mul | solution.py:581
  43.1 0.0 copy-done
  (1 shorter events, 0.0 us)
Async XLA Ops:
  42.3 0.8 %copy-start = (f32[16,16]{1,0:T(8,128)}, f32[16,16]{1,0:T(8,128)S(1)}, u32[]{:S(2)}) copy-start(f32[16,16]{1,0:T(8,128)S(1)} %broadcast_minimum_fusion) | copy-start | bytes 3076

commit v4 on v3

--- a/solution.py
+++ b/solution.py
@@ -11,6 +11,7 @@
 MESH = pl.DeviceIdType.MESH
 PITCH = 32
 BASE = 8
+UA, UY, UV, UC, UE4 = 2, 4, 7, 4, 4
 
 
 def strain_of(diffs, m):
@@ -22,7 +23,7 @@
 
 
 def kernel(sizes, vel, met, dm_out, line_out, half_out, U, O6, SY, RY, SC, RC, RO, ZG, SZX, RZX, SZY, RZY,
-           RZC, SZG, TZ, UE, ZE, VE, VHE, T, YF, YV, VH, MB, DM, LN, RX, RZ, lsem, ssem, rsem):
+           SZC, RZC, ZC, SZG, TZ, UE, ZE, VE, VHE, T, YF, YV, VH, MB, DM, NP, LN, RX, RZ, lsem, ssem, rsem):
     ngx, ngy, ngz = sizes
     nx = vel.shape[1]
     ny = vel.shape[2]
@@ -122,7 +123,7 @@
             def _():
                 RC[2 * s + q] = jnp.zeros(RC.shape[1:], F32)
                 for d in range(3):
-                    RZC[d, 2 * s + q] = z8
+                    RZC[d, 2 * s + q] = jnp.zeros(RZC.shape[2:], F32)
 
     for cp in ins:
         cp.wait()
@@ -175,41 +176,38 @@
                 acc = jnp.where(lx == X, pltpu.roll(a, (6 * X + 2) % 128, 1), acc)
             O6[f, 8 * t : 8 * t + 8, :] = acc
 
-    for s in range(2):
-        first = 6 * (nx if s else 2)
+    def x_at(f, t):
+        return 54 * t + (12 * f if f < 3 else 18 + 6 * f)
+
+    def x_lanes(lanes, at, f):
+        return jnp.logical_and(lanes >= at, lanes < at + (12 if f < 3 else 6))
+
+    for s in range(2):
+        acc = z8
         for t in range(2):
-            acc = z8
             for f in range(6):
-                part = pltpu.roll(O6[f, 8 * t : 8 * t + 8, :], (12 * f - first) % 128, 1)
-                acc = jnp.where(jnp.logical_and(lane >= 12 * f, lane < 12 * f + 12), part, acc)
-            SZX[s, 8 * t : 8 * t + 8, :] = acc
+                first = 6 * ((nx + (f >= 3)) if s else 2)
+                part = pltpu.roll(O6[f, 8 * t : 8 * t + 8, :], (x_at(f, t) - first) % 128, 1)
+                acc = jnp.where(x_lanes(lane, x_at(f, t), f), part, acc)
+        SZX[s] = acc
+        for sy in range(2):
+            for k in range(2):
+                SZC[2 * s + sy, k] = acc[6 + k : 7 + k] if sy else acc[k : k + 1]
         y = ny - 2 if s else 0
         for f in range(6):
             SZY[s, 2 * f : 2 * f + 2, :] = O6[f, y : y + 2, :]
         SZY[s, 12:16, :] = z8[0:4]
 
-    def corner_rows(out, sx, sy):
-        r = 0
-        for f in range(6):
-            for kx in range(2):
-                for ky in range(2):
-                    if f >= 3 and (kx != sx or ky != sy):
-                        continue
-                    if out:
-                        X = (nx if sx else 2) + kx
-                        y = (ny - 2 if sy else 0) + ky
-                    else:
-                        X = (nx + 2 if sx else 0) + kx
-                        y = (ny if sy else -2) + ky
-                    yield r, f, X, y + BASE
-                    r += 1
+    def corner_rows(sx, sy):
+        rows = [(f, kx, ky) for f in range(6) for kx in range(2) for ky in range(2)
+                if (kx == sx and ky == sy) or (f < 3 and (kx == sx or ky == sy))]
+        return [(12 * zt + r, zt, *q) for zt in range(2) for r, q in enumerate(rows)]
 
     for sx in range(2):
         for sy in range(2):
-            for r, f, X, yr in corner_rows(True, sx, sy):
-                for zt in range(2):
-                    SC[2 * sx + sy, zt, r : r + 1, :] = U[f, zt, X, yr : yr + 1, :]
-
+            for r, zt, f, kx, ky in corner_rows(sx, sy):
+                X, yr = (nx if sx else 2) + kx, (ny - 2 if sy else 0) + ky + BASE
+                SC[2 * sx + sy, r : r + 1, :] = U[f, zt, X, yr : yr + 1, :]
 
     for s in range(2):
         put(s, O6, RO.at[1 - s], {"gz": gz_at(1 if s else -1)})
@@ -222,43 +220,65 @@
                 has["x", s], has["x", 1 - s])
         for sx in range(2):
             for sy in range(2):
-                put(24 + 4 * i + 2 * sx + sy, SZX.at[sx, pl.ds(ny - 8 if sy else 0, 8), :],
+                put(24 + 4 * i + 2 * sx + sy, SZC.at[2 * sx + sy],
                     RZC.at[o, 2 * (1 - sx) + 1 - sy],
                     {"gx": dx(sx), "gy": dy(sy), "gz": gz_at(d)},
                     both[sx, sy], both[1 - sx, 1 - sy])
     def comb(left, own, right):
         return jnp.where(lc < 2, left, jnp.where(lc == 2, own, pltpu.roll(jnp.where(lc == 1, own, right), 2, 1)))
 
-    for n in (0, 1, *range(12, 36)):
+    got(0)
+    got(1)
+    for n in (12,13,14,15,16,17):
         got(n)
-    zx, zc = {}, {}
+    rr = pl.ds(BASE, ny)
+    for s in range(2):
+        far, near = (nx, nx + 1) if s else (3, 2)
+        gfar, gnear = (0, 1) if s else (nx + 3, nx + 2)
+        put(4 + s, U.at[:, :, near, rr, :], U.at[:, :, gnear, rr, :], {"gx": dx(s)},
+            has["x", s], has["x", 1 - s])
+        put(6 + s, U.at[pl.ds(0, 3), :, far, rr, :], U.at[pl.ds(0, 3), :, gfar, rr, :],
+            {"gx": dx(s)}, has["x", s], has["x", 1 - s])
+    for sx in range(2):
+        for sy in range(2):
+            put(8 + 2 * sx + sy, SC.at[2 * sx + sy], RC.at[2 * (1 - sx) + 1 - sy],
+                {"gx": dx(sx), "gy": dy(sy)}, both[sx, sy], both[1 - sx, 1 - sy])
+    for n in range(18, 36):
+        got(n)
+    zx = [comb(RZX[0, s], RZX[1, s], RZX[2, s]) for s in range(2)]
     for s in range(2):
         for t in range(2):
             rows = slice(8 * t, 8 * t + 8)
-            zx[s, t] = comb(RZX[0, s, rows, :], RZX[1, s, rows, :], RZX[2, s, rows, :])
             SZG[s, rows, :] = comb(RZY[0, s, rows, :], RZY[1, s, rows, :], RZY[2, s, rows, :])
+    lane1 = lc[0:1]
     for c in range(4):
-        zc[c] = comb(RZC[0, c], RZC[1, c], RZC[2, c])
+        ZC[c] = z8
+        for k in range(2):
+            left, own, right = (RZC[d, c, k] for d in range(3))
+            ZC[c, k : k + 1, :] = jnp.where(lane1 < 2, left, jnp.where(
+                lane1 == 2, own, pltpu.roll(jnp.where(lane1 == 1, own, right), 2, 1)))
+
+    def x_place(sx, f):
+        return 6 * (nx + 2) if sx else (0 if f < 3 else 6)
+
     for f in range(6):
         ZG[f, 0:8, :] = z8
         ZG[f, 24:32, :] = z8
         for t in range(2):
             rows = slice(8 * t, 8 * t + 8)
             z = comb(RO[0, f, rows, :], O6[f, rows, :], RO[1, f, rows, :])
-            for s in range(2):
-                at = 6 * (nx + 2) if s else 0
-                part = pltpu.roll(zx[s, t], (at - 12 * f) % 128, 1)
-                z = jnp.where(jnp.logical_and(lane >= at, lane < at + 12), part, z)
+            for sx in range(2):
+                at = x_place(sx, f)
+                part = pltpu.roll(zx[sx], (at - x_at(f, t)) % 128, 1)
+                z = jnp.where(x_lanes(lane, at, f), part, z)
             ZG[f, BASE + 8 * t : BASE + 8 * t + 8, :] = z
         for sy in range(2):
             yr = BASE + (ny if sy else -2)
             z = SZG[sy, 2 * f : 2 * f + 2, :]
             for sx in range(2):
-                at = 6 * (nx + 2) if sx else 0
-                part = pltpu.roll(zc[2 * sx + sy], (at - 12 * f) % 128, 1)
-                part = part[0:2] if sy else part[6:8]
-                lane2 = lane[0:2]
-                z = jnp.where(jnp.logical_and(lane2 >= at, lane2 < at + 12), part, z)
+                at = x_place(sx, f)
+                part = pltpu.roll(ZC[2 * sx + sy], (at - x_at(f, 1 - sy)) % 128, 1)[0:2]
+                z = jnp.where(x_lanes(lane[0:2], at, f), part, z)
             ZG[f, yr : yr + 2, :] = z
 
     def edge(a):
@@ -391,26 +411,20 @@
                 num = n_ if num is None else num + n_
                 den = d_ if den is None else den + d_
                 DM[X - 2, zt, r : r + 8, :] = delta * MB[X, zt, r + 1 : r + 9, :]
-            at = X - 2 + nx * t
-            ln = jnp.where(lane == at, jnp.sum(num, axis=1, keepdims=True), LN[gz])
-            LN[gz] = jnp.where(lane == at + 2 * nx, jnp.sum(den, axis=1, keepdims=True), ln)
+            NP[0, X - 2, r : r + 8, :] = num
+            NP[1, X - 2, r : r + 8, :] = den
         return 0
 
-    LN[gz] = z8
+    def line_sums(acc, planes):
+        for x in planes:
+            for t in range(2):
+                for k in range(2):
+                    part = jnp.sum(NP[k, x, 8 * t : 8 * t + 8, :], axis=1, keepdims=True)
+                    acc = jnp.where(lane == x + nx * t + 2 * nx * k, part, acc)
+        return acc
+
     got(2)
     got(3)
-    rr = pl.ds(BASE, ny)
-    for s in range(2):
-        far, near = (nx, nx + 1) if s else (3, 2)
-        gfar, gnear = (0, 1) if s else (nx + 3, nx + 2)
-        put(4 + s, U.at[:, :, near, rr, :], U.at[:, :, gnear, rr, :], {"gx": dx(s)},
-            has["x", s], has["x", 1 - s])
-        put(6 + s, U.at[pl.ds(0, 3), :, far, rr, :], U.at[pl.ds(0, 3), :, gfar, rr, :],
-            {"gx": dx(s)}, has["x", s], has["x", 1 - s])
-    for sx in range(2):
-        for sy in range(2):
-            put(8 + 2 * sx + sy, SC.at[2 * sx + sy], RC.at[2 * (1 - sx) + 1 - sy],
-                {"gx": dx(sx), "gy": dy(sy)}, both[sx, sy], both[1 - sx, 1 - sy])
 
     for s in range(2):
         for f in range(6):
@@ -421,37 +435,29 @@
                 slab = 2 * f + k if f < 3 else 3 + f
                 for zt in range(2):
                     U[f, zt, pl.ds(2, nx), BASE + y, :] = RY[s, slab, zt, :, :]
-    lax.fori_loop(3, nx + 1, stage_a, 0)
-    lax.fori_loop(2, nx + 2, stage_y, 0)
-    lax.fori_loop(3, nx + 1, stage_v, 0)
-    lax.fori_loop(4, nx, stage_c, 0)
+    lax.fori_loop(3, nx + 1, stage_a, 0, unroll=UA)
+    lax.fori_loop(2, nx + 2, stage_y, 0, unroll=UY)
+    lax.fori_loop(3, nx + 1, stage_v, 0, unroll=UV)
+    lax.fori_loop(4, nx, stage_c, 0, unroll=UC)
+
+    sums = line_sums(z8, range(2, nx - 2))
 
     for n in range(4, 12):
         got(n)
     for sx in range(2):
         for sy in range(2):
-            src = {}
-            r = 0
-            for f in range(6):
-                for kx in range(2):
-                    for ky in range(2):
-                        if f >= 3 and (kx != 1 - sx or ky != 1 - sy):
-                            continue
-                        src[f, kx, ky] = r
-                        r += 1
-            for (f, kx, ky), r in src.items():
-                X = (nx + 2 if sx else 0) + kx
-                yr = (ny if sy else -2) + ky + BASE
-                for zt in range(2):
-                    U[f, zt, X, yr : yr + 1, :] = RC[2 * sx + sy, zt, r : r + 1, :]
+            for r, zt, f, kx, ky in corner_rows(1 - sx, 1 - sy):
+                X, yr = (nx + 2 if sx else 0) + kx, (ny if sy else -2) + ky + BASE
+                U[f, zt, X, yr : yr + 1, :] = RC[2 * sx + sy, r : r + 1, :]
 
     def ends(a, stage):
-        lax.fori_loop(0, 4, lambda k, c: stage(jnp.where(k < 2, a + k, nx - a + k), c), 0)
+        lax.fori_loop(0, 4, lambda k, c: stage(jnp.where(k < 2, a + k, nx - a + k), c), 0, unroll=UE4)
 
     ends(1, stage_a)
     ends(0, stage_y)
     ends(1, stage_v)
     ends(2, stage_c)
+    LN[gz] = line_sums(sums, (0, 1, nx - 2, nx - 1))
 
     outs = []
     for zt in range(2):
@@ -547,15 +553,17 @@
                 vm(6, 16, 128),
                 vm(2, 9, 2, nx, 128),
                 vm(2, 9, 2, nx, 128),
-                vm(4, 2, 16, 128),
-                vm(4, 2, 16, 128),
+                vm(4, 24, 128),
+                vm(4, 24, 128),
                 vm(2, 6, 16, 128),
                 vm(6, 32, 128),
+                vm(2, 8, 128),
+                vm(3, 2, 8, 128),
                 vm(2, 16, 128),
                 vm(3, 2, 16, 128),
-                vm(2, 16, 128),
-                vm(3, 2, 16, 128),
-                vm(3, 4, 8, 128),
+                vm(4, 2, 1, 128),
+                vm(3, 4, 2, 1, 128),
+                vm(4, 8, 128),
                 vm(2, 16, 128),
                 vm(12, 24, 128),
                 vm(3, 24, 128),
@@ -568,6 +576,7 @@
                 vm(3, 2, nx + 4, 24, 128),
                 vm(nx + 4, 2, 24, 128),
                 vm(nx, 2, 16, 128),
+                vm(2, nx, 16, 128),
                 vm(ngz, 8, 128),
                 vm(2 * ngy, 1, 128),
                 vm(ngx // 2, 1, 128),

time: 43.2 us -> 38.1 us (0.88)
  Pallas kernels: 41.6 us -> 36.5 us
    pallas_call x1, Pallas kernels: 41.6 us -> 36.5 us  [per_device(): pl.pallas_call(functools.partial(kernel, sizes), out_shape=(vm(nx, ny, nz...]
where the time goes in v4:
time: 38.1 us; the launch traced here: 38 us
  Pallas kernels  36.5 us (96%)
  other arithmetic  0.84 us (2%)
  between operations  0.65 us (2%)
    pallas_call x1, Pallas kernels, per_device(): pl.pallas_call(functools.partial(kernel, sizes), out_shape=(vm(nx, ny, nz...  36.5 us
    mul x1, other arithmetic, per_device(): return (coefficient[:, :, None] * dm, coefficient)  0.81 us

profile of v4, /device:TPU:1, one launch (start us, length us, event | category | flops | bytes accessed | tf_op | source)
XLA Modules:
  0.0 38.0 jit_solution(4921876239489202697)
XLA Ops:
  0.6 36.5 %shard_map.41 = (f32[16,16,256]{2,1,0:T(8,128)S(1)}, f32[16,16]{1,0:T(8,128)S(1)}, f32[1,128]{1,0:T(1,128)S(1)}) custom-call(f32[3,16,16,256]{3,2,1,0:T(8,128)} %vel.1, f32[3,16,16,256]{3,2,1,0:T(8,128)} %met.1), custom_call_target="tpu_custom_call" | custom-call | tf_op jit(solution)/shard_map/pallas_call | solution.py:546
  37.2 0.0 copy-start
  37.2 0.8 %broadcast_multiply_fusion = f32[16,16,256]{2,1,0:T(8,128)} fusion(f32[16,16,256]{2,1,0:T(8,128)S(1)} %get-tuple-element.7, f32[16,16]{1,0:T(8,128)S(1)} %broadcast_minimum_fusion), kind=kLoop, calls=%fused_computation | loop fusion | flops 65536 | bytes 525312 | tf_op jit(solution)/shard_map/mul | solution.py:590
  38.0 0.0 copy-done
  (1 shorter events, 0.0 us)
Async XLA Ops:
  37.2 0.8 %copy-start = (f32[16,16]{1,0:T(8,128)}, f32[16,16]{1,0:T(8,128)S(1)}, u32[]{:S(2)}) copy-start(f32[16,16]{1,0:T(8,128)S(1)} %broadcast_minimum_fusion) | copy-start | bytes 3076

commit v5 on v4

--- a/solution.py
+++ b/solution.py
@@ -23,14 +23,12 @@
 
 
 def kernel(sizes, vel, met, dm_out, line_out, half_out, U, O6, SY, RY, SC, RC, RO, ZG, SZX, RZX, SZY, RZY,
-           SZC, RZC, ZC, SZG, TZ, UE, ZE, VE, VHE, T, YF, YV, VH, MB, DM, NP, LN, RX, RZ, lsem, ssem, rsem):
+           SZC, RZC, ZC, SZG, TZ, UE, ZE, VE, VHE, T, YF, YV, VH, MB, DM, NP, LN, RX, lsem, ssem, rsem):
     ngx, ngy, ngz = sizes
     nx = vel.shape[1]
     ny = vel.shape[2]
     nz = vel.shape[3]
     gx, gy, gz = lax.axis_index("gx"), lax.axis_index("gy"), lax.axis_index("gz")
-    nzc = ngx // 2
-    xlo, xz = lax.rem(gx, 2), lax.div(gx, 2)
     has = {("x", 0): gx > 0, ("x", 1): gx < ngx - 1, ("y", 0): gy > 0, ("y", 1): gy < ngy - 1}
 
     ins = []
@@ -78,27 +76,25 @@
                 for d in (-1, 0, 1):
                     greet({"gx": dx(s), "gy": dy(q), "gz": gz_at(d)})
 
-    for k in range(2, ngz - 1):
-        greet({"gz": gz_at(k)})
-
-    nxc = 2 * ngy
-    me_c = xlo * ngy + gy
-
-    def xc_dev(k):
-        c = lax.rem(me_c + k, nxc)
-        return c, {"gx": xz * 2 + lax.div(c, ngy), "gy": lax.rem(c, ngy)}
-
-    def z_dev(k):
-        c = lax.rem(xz + k, nzc)
-        return c, {"gx": c * 2 + xlo}
-
-    for k in range(1, nxc):
-        greet(xc_dev(k)[1])
-    for k in range(1, nzc):
-        greet(z_dev(k)[1])
+    core, xhi, nhi = lax.rem(gy, 2), lax.div(gy, 2), ngy // 2
+    n1, n2 = 2 * ngz, ngx * nhi
+    me1, me2 = core * ngz + gz, gx * nhi + xhi
+
+    def dev1(k):
+        c = lax.rem(me1 + k, n1)
+        return c, {"gy": 2 * xhi + lax.div(c, ngz), "gz": lax.rem(c, ngz)}
+
+    def dev2(k):
+        c = lax.rem(me2 + k, n2)
+        return c, {"gx": lax.div(c, nhi), "gy": 2 * lax.rem(c, nhi) + core}
+
+    for k in range(1, n1):
+        greet(dev1(k)[1])
+    for k in range(1, n2):
+        greet(dev2(k)[1])
     ex = has["x", 0].astype(jnp.int32) + has["x", 1].astype(jnp.int32)
     ey = has["y", 0].astype(jnp.int32) + has["y", 1].astype(jnp.int32)
-    partners = 3 * (1 + ex) * (1 + ey) - 1 + max(ngz - 3, 0) + (nxc - 1) + (nzc - 1)
+    partners = 3 * (1 + ex) * (1 + ey) - 1 + n1 - 1 + n2 - 1
 
     z8 = jnp.zeros((8, 128), F32)
     for s in range(2):
@@ -224,6 +220,10 @@
                     RZC.at[o, 2 * (1 - sx) + 1 - sy],
                     {"gx": dx(sx), "gy": dy(sy), "gz": gz_at(d)},
                     both[sx, sy], both[1 - sx, 1 - sy])
+    for sx in range(2):
+        for sy in range(2):
+            put(8 + 2 * sx + sy, SC.at[2 * sx + sy], RC.at[2 * (1 - sx) + 1 - sy],
+                {"gx": dx(sx), "gy": dy(sy)}, both[sx, sy], both[1 - sx, 1 - sy])
     def comb(left, own, right):
         return jnp.where(lc < 2, left, jnp.where(lc == 2, own, pltpu.roll(jnp.where(lc == 1, own, right), 2, 1)))
 
@@ -239,10 +239,6 @@
             has["x", s], has["x", 1 - s])
         put(6 + s, U.at[pl.ds(0, 3), :, far, rr, :], U.at[pl.ds(0, 3), :, gfar, rr, :],
             {"gx": dx(s)}, has["x", s], has["x", 1 - s])
-    for sx in range(2):
-        for sy in range(2):
-            put(8 + 2 * sx + sy, SC.at[2 * sx + sy], RC.at[2 * (1 - sx) + 1 - sy],
-                {"gx": dx(sx), "gy": dy(sy)}, both[sx, sy], both[1 - sx, 1 - sy])
     for n in range(18, 36):
         got(n)
     zx = [comb(RZX[0, s], RZX[1, s], RZX[2, s]) for s in range(2)]
@@ -457,7 +453,7 @@
     ends(0, stage_y)
     ends(1, stage_v)
     ends(2, stage_c)
-    LN[gz] = line_sums(sums, (0, 1, nx - 2, nx - 1))
+    LN[me1] = line_sums(sums, (0, 1, nx - 2, nx - 1))
 
     outs = []
     for zt in range(2):
@@ -466,59 +462,38 @@
         outs.append(cp)
 
     cps = []
-    for k in range(1, ngz):
-        cp = pltpu.make_async_remote_copy(
-            src_ref=LN.at[gz], dst_ref=LN.at[gz], send_sem=ssem.at[40 + k], recv_sem=rsem.at[40 + gz],
-            device_id={"gz": lax.rem(gz + k, ngz)}, device_id_type=MESH)
-        cp.start()
-        cps.append(cp)
-    for k in range(1, ngz):
-        src = lax.rem(gz + k, ngz)
-        pltpu.make_async_remote_copy(
-            src_ref=LN.at[gz], dst_ref=LN.at[src], send_sem=ssem.at[40 + k], recv_sem=rsem.at[40 + src],
-            device_id={"gz": src}, device_id_type=MESH).wait_recv()
-    tot = LN[0]
-    for k in range(1, ngz):
-        tot = tot + LN[k]
-    tot = tot * (1.0 / (nz * ngz))
-    den = pltpu.roll(tot, 128 - 2 * nx, 1)
-    line = tot / (den + 1e-06)
-    valid = lane < 2 * nx
-    peak = jnp.max(jnp.where(valid, line, -jnp.inf), axis=0, keepdims=True)
-    peak = jnp.max(peak, axis=1, keepdims=True)
-
-    RX[me_c] = jnp.broadcast_to(peak, (1, 128))
-    for k in range(1, nxc):
-        c, dev = xc_dev(k)
-        cp = pltpu.make_async_remote_copy(
-            src_ref=RX.at[me_c], dst_ref=RX.at[me_c], send_sem=ssem.at[44 + k], recv_sem=rsem.at[44 + me_c],
-            device_id=dev, device_id_type=MESH)
-        cp.start()
-        cps.append(cp)
-    for k in range(1, nxc):
-        c, dev = xc_dev(k)
-        pltpu.make_async_remote_copy(
-            src_ref=RX.at[me_c], dst_ref=RX.at[c], send_sem=ssem.at[44 + k], recv_sem=rsem.at[44 + c],
-            device_id=dev, device_id_type=MESH).wait_recv()
+
+    def spread(ref, me, n, dev, at):
+        def copy(k, c):
+            return pltpu.make_async_remote_copy(
+                src_ref=ref.at[me], dst_ref=ref.at[c], send_sem=ssem.at[at + k], recv_sem=rsem.at[at + c],
+                device_id=dev(k)[1], device_id_type=MESH)
+
+        for k in range(1, n):
+            cp = copy(k, me)
+            cp.start()
+            cps.append(cp)
+        for k in range(1, n):
+            copy(k, dev(k)[0]).wait_recv()
+
+    spread(LN, me1, n1, dev1, 36)
+
+    def line_of(q):
+        tot = LN[q * ngz]
+        for k in range(1, ngz):
+            tot = tot + LN[q * ngz + k]
+        tot = tot * (1.0 / (nz * ngz))
+        return tot / (pltpu.roll(tot, 128 - 2 * nx, 1) + 1e-06)
+
+    peak = jnp.where(lane < 2 * nx, jnp.maximum(line_of(0), line_of(1)), -jnp.inf)
+    peak = jnp.max(jnp.max(peak, axis=0, keepdims=True), axis=1, keepdims=True)
+
+    RX[me2] = jnp.broadcast_to(peak, (1, 128))
+    spread(RX, me2, n2, dev2, 36 + n1)
     peak = RX[0]
-    for k in range(1, nxc):
+    for k in range(1, n2):
         peak = jnp.maximum(peak, RX[k])
-    RZ[xz] = peak
-    for k in range(1, nzc):
-        c, dev = z_dev(k)
-        cp = pltpu.make_async_remote_copy(
-            src_ref=RZ.at[xz], dst_ref=RZ.at[xz], send_sem=ssem.at[52 + k], recv_sem=rsem.at[52 + xz],
-            device_id=dev, device_id_type=MESH)
-        cp.start()
-        cps.append(cp)
-    for k in range(1, nzc):
-        c, dev = z_dev(k)
-        pltpu.make_async_remote_copy(
-            src_ref=RZ.at[xz], dst_ref=RZ.at[c], send_sem=ssem.at[52 + k], recv_sem=rsem.at[52 + c],
-            device_id=dev, device_id_type=MESH).wait_recv()
-    peak = RZ[0]
-    for k in range(1, nzc):
-        peak = jnp.maximum(peak, RZ[k])
+    line = line_of(core)
 
     half_out[...] = 0.5 * peak
     lt = line.T
@@ -577,12 +552,11 @@
                 vm(nx + 4, 2, 24, 128),
                 vm(nx, 2, 16, 128),
                 vm(2, nx, 16, 128),
-                vm(ngz, 8, 128),
-                vm(2 * ngy, 1, 128),
-                vm(ngx // 2, 1, 128),
+                vm(2 * ngz, 8, 128),
+                vm(ngx * ngy // 2, 1, 128),
                 pltpu.SemaphoreType.DMA((6,)),
-                pltpu.SemaphoreType.DMA((60,)),
-                pltpu.SemaphoreType.DMA((60,)),
+                pltpu.SemaphoreType.DMA((36 + 2 * ngz + ngx * ngy // 2,)),
+                pltpu.SemaphoreType.DMA((36 + 2 * ngz + ngx * ngy // 2,)),
             ],
             compiler_params=pltpu.CompilerParams(collective_id=0, has_side_effects=True),
         )(velocity, metric)

time: 38.1 us -> 37 us (0.971)
  Pallas kernels: 36.5 us -> 35.4 us
    pallas_call x1, Pallas kernels: 36.5 us -> 35.4 us  [per_device(): pl.pallas_call(functools.partial(kernel, sizes), out_shape=(vm(nx, ny, nz...]
where the time goes in v5:
time: 37 us; the launch traced here: 36.9 us
  Pallas kernels  35.4 us (96%)
  other arithmetic  0.84 us (2%)
  between operations  0.65 us (2%)
    pallas_call x1, Pallas kernels, per_device(): pl.pallas_call(functools.partial(kernel, sizes), out_shape=(vm(nx, ny, nz...  35.4 us
    mul x1, other arithmetic, per_device(): return (coefficient[:, :, None] * dm, coefficient)  0.81 us

profile of v5, /device:TPU:1, one launch (start us, length us, event | category | flops | bytes accessed | tf_op | source)
XLA Modules:
  0.0 36.9 jit_solution(15431981618316560963)
XLA Ops:
  0.6 35.4 %shard_map.41 = (f32[16,16,256]{2,1,0:T(8,128)S(1)}, f32[16,16]{1,0:T(8,128)S(1)}, f32[1,128]{1,0:T(1,128)S(1)}) custom-call(f32[3,16,16,256]{3,2,1,0:T(8,128)} %vel.1, f32[3,16,16,256]{3,2,1,0:T(8,128)} %met.1), custom_call_target="tpu_custom_call" | custom-call | tf_op jit(solution)/shard_map/pallas_call | solution.py:521
  36.1 0.0 copy-start
  36.1 0.8 %broadcast_multiply_fusion = f32[16,16,256]{2,1,0:T(8,128)} fusion(f32[16,16,256]{2,1,0:T(8,128)S(1)} %get-tuple-element.7, f32[16,16]{1,0:T(8,128)S(1)} %broadcast_minimum_fusion), kind=kLoop, calls=%fused_computation | loop fusion | flops 65536 | bytes 525312 | tf_op jit(solution)/shard_map/mul | solution.py:564
  36.9 0.0 copy-done
  (1 shorter events, 0.0 us)
Async XLA Ops:
  36.1 0.8 %copy-start = (f32[16,16]{1,0:T(8,128)}, f32[16,16]{1,0:T(8,128)S(1)}, u32[]{:S(2)}) copy-start(f32[16,16]{1,0:T(8,128)S(1)} %broadcast_minimum_fusion) | copy-start | bytes 3076

commit v6 on v5

--- a/solution.py
+++ b/solution.py
@@ -438,7 +438,7 @@
 
     sums = line_sums(z8, range(2, nx - 2))
 
-    for n in range(4, 12):
+    for n in range(8, 12):
         got(n)
     for sx in range(2):
         for sy in range(2):
@@ -446,6 +446,8 @@
                 X, yr = (nx + 2 if sx else 0) + kx, (ny if sy else -2) + ky + BASE
                 U[f, zt, X, yr : yr + 1, :] = RC[2 * sx + sy, r : r + 1, :]
 
+    for n in range(4, 8):
+        got(n)
     def ends(a, stage):
         lax.fori_loop(0, 4, lambda k, c: stage(jnp.where(k < 2, a + k, nx - a + k), c), 0, unroll=UE4)
 
@@ -463,20 +465,25 @@
 
     cps = []
 
-    def spread(ref, me, n, dev, at):
+    def spread(ref, me, n, dev, at, order, meanwhile=None):
         def copy(k, c):
             return pltpu.make_async_remote_copy(
                 src_ref=ref.at[me], dst_ref=ref.at[c], send_sem=ssem.at[at + k], recv_sem=rsem.at[at + c],
                 device_id=dev(k)[1], device_id_type=MESH)
 
-        for k in range(1, n):
+        for k in order:
             cp = copy(k, me)
             cp.start()
             cps.append(cp)
-        for k in range(1, n):
+        if meanwhile is not None:
+            meanwhile()
+        for k in reversed(order):
             copy(k, dev(k)[0]).wait_recv()
 
-    spread(LN, me1, n1, dev1, 36)
+    def far_first(n, span):
+        return sorted(range(1, n), key=lambda k: -min(k % span, span - k % span))
+
+    spread(LN, me1, n1, dev1, 36, far_first(n1, ngz))
 
     def line_of(q):
         tot = LN[q * ngz]
@@ -489,26 +496,26 @@
     peak = jnp.max(jnp.max(peak, axis=0, keepdims=True), axis=1, keepdims=True)
 
     RX[me2] = jnp.broadcast_to(peak, (1, 128))
-    spread(RX, me2, n2, dev2, 36 + n1)
+
+    def while_peak_travels():
+        lt = line_of(core).T
+        for t in range(2):
+            line_out[:, 8 * t : 8 * t + 8] = lt[nx * t : nx * t + nx, :]
+        for cp in outs:
+            cp.wait()
+        for cp in cps:
+            cp.wait_send()
+        for cp, cond in waits_send:
+            if cond is None:
+                cp.wait_send()
+            else:
+                pl.when(cond)(cp.wait_send)
+
+    spread(RX, me2, n2, dev2, 36 + n1, far_first(n2, n2), while_peak_travels)
     peak = RX[0]
     for k in range(1, n2):
         peak = jnp.maximum(peak, RX[k])
-    line = line_of(core)
-
     half_out[...] = 0.5 * peak
-    lt = line.T
-    for t in range(2):
-        line_out[:, 8 * t : 8 * t + 8] = lt[nx * t : nx * t + nx, :]
-    for cp in outs:
-        cp.wait()
-
-    for cp in cps:
-        cp.wait_send()
-    for cp, cond in waits_send:
-        if cond is None:
-            cp.wait_send()
-        else:
-            pl.when(cond)(cp.wait_send)
 
 
 def solution(mesh):

time: 37 us -> 36.6 us (0.989)
  Pallas kernels: 35.4 us -> 35 us
    pallas_call x1, Pallas kernels: 35.4 us -> 35 us  [per_device(): pl.pallas_call(functools.partial(kernel, sizes), out_shape=(vm(nx, ny, nz...]
where the time goes in v6:
time: 36.6 us; the launch traced here: 36.5 us
  Pallas kernels  35 us (96%)
  other arithmetic  0.84 us (2%)
  between operations  0.65 us (2%)
    pallas_call x1, Pallas kernels, per_device(): pl.pallas_call(functools.partial(kernel, sizes), out_shape=(vm(nx, ny, nz...  35 us
    mul x1, other arithmetic, per_device(): return (coefficient[:, :, None] * dm, coefficient)  0.81 us

profile of v6, /device:TPU:1, one launch (start us, length us, event | category | flops | bytes accessed | tf_op | source)
XLA Modules:
  0.0 36.5 jit_solution(12297469865578934862)
XLA Ops:
  0.6 35.0 %shard_map.41 = (f32[16,16,256]{2,1,0:T(8,128)S(1)}, f32[16,16]{1,0:T(8,128)S(1)}, f32[1,128]{1,0:T(1,128)S(1)}) custom-call(f32[3,16,16,256]{3,2,1,0:T(8,128)} %vel.1, f32[3,16,16,256]{3,2,1,0:T(8,128)} %met.1), custom_call_target="tpu_custom_call" | custom-call | tf_op jit(solution)/shard_map/pallas_call | solution.py:528
  35.6 0.0 copy-start
  35.7 0.8 %broadcast_multiply_fusion = f32[16,16,256]{2,1,0:T(8,128)} fusion(f32[16,16,256]{2,1,0:T(8,128)S(1)} %get-tuple-element.7, f32[16,16]{1,0:T(8,128)S(1)} %broadcast_minimum_fusion), kind=kLoop, calls=%fused_computation | loop fusion | flops 65536 | bytes 525312 | tf_op jit(solution)/shard_map/mul | solution.py:571
  36.5 0.0 copy-done
  (1 shorter events, 0.0 us)
Async XLA Ops:
  35.6 0.8 %copy-start = (f32[16,16]{1,0:T(8,128)}, f32[16,16]{1,0:T(8,128)S(1)}, u32[]{:S(2)}) copy-start(f32[16,16]{1,0:T(8,128)S(1)} %broadcast_minimum_fusion) | copy-start | bytes 3076

commit v7 on v6

--- a/solution.py
+++ b/solution.py
@@ -11,7 +11,7 @@
 MESH = pl.DeviceIdType.MESH
 PITCH = 32
 BASE = 8
-UA, UY, UV, UC, UE4 = 2, 4, 7, 4, 4
+UA, UY, UV, UC, UE4 = 7, 4, 7, 6, 4
 
 
 def strain_of(diffs, m):

time: 36.6 us -> 36.6 us (level)
  no operation moved by 1% of the time
where the time goes in v7:
time: 36.6 us; the launch traced here: 36.5 us
  Pallas kernels  35 us (96%)
  other arithmetic  0.84 us (2%)
  between operations  0.65 us (2%)
    pallas_call x1, Pallas kernels, per_device(): pl.pallas_call(functools.partial(kernel, sizes), out_shape=(vm(nx, ny, nz...  35 us
    mul x1, other arithmetic, per_device(): return (coefficient[:, :, None] * dm, coefficient)  0.81 us

profile of v7, /device:TPU:1, one launch (start us, length us, event | category | flops | bytes accessed | tf_op | source)
XLA Modules:
  0.0 36.5 jit_solution(10773140340199187588)
XLA Ops:
  0.6 35.0 %shard_map.41 = (f32[16,16,256]{2,1,0:T(8,128)S(1)}, f32[16,16]{1,0:T(8,128)S(1)}, f32[1,128]{1,0:T(1,128)S(1)}) custom-call(f32[3,16,16,256]{3,2,1,0:T(8,128)} %vel.1, f32[3,16,16,256]{3,2,1,0:T(8,128)} %met.1), custom_call_target="tpu_custom_call" | custom-call | tf_op jit(solution)/shard_map/pallas_call | solution.py:528
  35.6 0.0 copy-start
  35.7 0.8 %broadcast_multiply_fusion = f32[16,16,256]{2,1,0:T(8,128)} fusion(f32[16,16,256]{2,1,0:T(8,128)S(1)} %get-tuple-element.7, f32[16,16]{1,0:T(8,128)S(1)} %broadcast_minimum_fusion), kind=kLoop, calls=%fused_computation | loop fusion | flops 65536 | bytes 525312 | tf_op jit(solution)/shard_map/mul | solution.py:571
  36.5 0.0 copy-done
  (1 shorter events, 0.0 us)
Async XLA Ops:
  35.6 0.8 %copy-start = (f32[16,16]{1,0:T(8,128)}, f32[16,16]{1,0:T(8,128)S(1)}, u32[]{:S(2)}) copy-start(f32[16,16]{1,0:T(8,128)S(1)} %broadcast_minimum_fusion) | copy-start | bytes 3076
